TPU v7x, 32 devices: a whole 2x2x4 slice. The times are simulated.
32 devices in a mesh: dp: 2 (over x), tp: 4 (over z), sp: 4 (over y, core).
Axes of the slice: x: 2, y: 2, z: 4, core: 2. Of those that a mesh axis runs over, the one named last changes fastest.
Arguments:
- hidden: bfloat16 [128, 3072], P('dp'), parts along dimension 0
- positions: int32 [128], P('dp'), parts along dimension 0
- k_cache: bfloat16 [2, 128, 512, 8, 128], P(None, 'dp', 'sp', 'tp'), parts along dimension 1
- v_cache: bfloat16 [2, 128, 512, 8, 128], P(None, 'dp', 'sp', 'tp'), parts along dimension 1
- ln_gain: bfloat16 [2, 2, 3072], replicated
- ln_bias: bfloat16 [2, 2, 3072], replicated
- w_qkv: bfloat16 [2, 3072, 5120], P(None, None, 'tp')
- b_qkv: bfloat16 [2, 5120], P(None, 'tp')
- w_dense: bfloat16 [2, 3072, 3072], P(None, 'tp')
- b_dense: bfloat16 [2, 3072], replicated
- w_up: bfloat16 [2, 3072, 16384], P(None, None, 'tp')
- b_up: bfloat16 [2, 16384], P(None, 'tp')
- w_down: bfloat16 [2, 8192, 3072], P(None, 'tp')
- b_down: bfloat16 [2, 3072], replicated
Outputs:
- output 1: bfloat16 [128, 3072], P('dp'), parts along dimension 0
- output 2: bfloat16 [2, 128, 512, 8, 128], P(None, 'dp', 'sp', 'tp'), parts along dimension 1
- output 3: bfloat16 [2, 128, 512, 8, 128], P(None, 'dp', 'sp', 'tp'), parts along dimension 1
There are 2 independent parts. A program takes and returns all parts, laid end to end along the dimension named above; an argument that names none is the same for every part.
All inputs are finite; a program needn't handle non-finite values.
Results may differ from a plain program's by a relative error of at most 0.017103.
Values sent between devices are 32-bit elements.
A program may use at most 1 GiB of HBM per device.

v0:
```python
import functools

import jax
import jax.numpy as jnp
import numpy as np
from jax import lax
from jax.experimental import pallas as pl
from jax.experimental.pallas import tpu as pltpu
from jax.sharding import PartitionSpec as P

MESH = pl.DeviceIdType.MESH
F32 = jnp.float32
BF16 = jnp.bfloat16
BLOCK_SIZE = 64
LOCAL_BLOCKS = 16
VERT_STRIDE = 8
ROPE_THETA = 1000000.0
GELU_LIMIT = 20.0
NORM_EPS = 0.00001
MASKED = -1e30

SEQS = 64
ROWS = 16
OWN = 4
SEQ_LEN = 512
SLOTS = 128
D = 3072
HEAD = 128
KV = 2
GROUP = 3
HEADS = KV * GROUP
QKV = 1280
UP = 4096
FF = 2048
STAT = HEADS * HEAD + HEAD
NCH = 3
CH = D // NCH
GRP = 8
NGRP = SEQS // GRP
VMEM_MAX = 67043328


def rope_tables():
    half = HEAD // 2
    inv = (ROPE_THETA ** (-np.arange(half).astype(np.float32) * np.float32(2.0 / HEAD))).astype(np.float32)
    angle = (np.arange(SEQ_LEN).astype(np.float32)[:, None] * inv[None, :]).astype(np.float64)
    cos, sin = np.cos(angle).astype(np.float32), np.sin(angle).astype(np.float32)
    return np.concatenate([cos, cos], 1), np.concatenate([-sin, sin], 1)


def norm_rows(wide, gain, shift):
    mean = jnp.mean(wide, axis=-1, keepdims=True)
    centred = wide - mean
    var = jnp.mean(centred * centred, axis=-1, keepdims=True)
    return (centred * lax.rsqrt(var + NORM_EPS) * gain + shift).astype(BF16)


def param_row(ref, layer, which=None):
    rows = ref[...] if which is None else ref[layer]
    pick = layer if which is None else which
    return rows.astype(F32)[pick:pick + 1]


def round_bf16(x):
    return x.astype(BF16).astype(F32)


def dot(a, b):
    return jnp.dot(a, b, preferred_element_type=F32)


def turn_columns(ref, rows, cos, sin):
    for c in range(KV):
        for g in range(GROUP + 2):
            cols = slice((c * 5 + g) * HEAD, (c * 5 + g + 1) * HEAD)
            x = ref[rows, cols]
            if g <= GROUP:
                x = x * cos + pltpu.roll(x, HEAD // 2, 1) * sin
            ref[rows, cols] = round_bf16(x)


def attend(group, sparse, pos_ref, q8, kbuf, vbuf, acc8, m8, l8):
    t, s = lax.axis_index("tp"), lax.axis_index("sp")
    row = lax.broadcasted_iota(jnp.int32, (8, 2 * SLOTS), 0)
    col = lax.broadcasted_iota(jnp.int32, (8, 2 * SLOTS), 1)
    slot = s * SLOTS + col // KV
    same = (col % KV) == row // GROUP
    vertical = (slot // BLOCK_SIZE + (t * HEADS + row) + 1) % VERT_STRIDE == 0
    for j in range(GRP):
        b = group * GRP + j
        p = pos_ref[b]
        at = pl.ds(pl.multiple_of(b * 8, 8), 8)
        scores = lax.dot_general(q8[at, :].astype(BF16), kbuf[b], (((1,), (1,)), ((), ())), preferred_element_type=F32)
        scores = scores * (1.0 / HEAD)
        keep = (slot < p) & same
        if sparse:
            near = (p // BLOCK_SIZE - slot // BLOCK_SIZE) < LOCAL_BLOCKS
            keep = keep & (near | vertical)
        scores = jnp.where(keep, scores, MASKED)
        peak = jnp.max(scores, axis=-1, keepdims=True)
        weights = jnp.where(keep, jnp.exp(scores - peak), 0.0)
        total = jnp.sum(weights, axis=-1, keepdims=True)
        acc8[at, :] = dot(weights.astype(BF16), vbuf[b])
        m8[at, :] = jnp.broadcast_to(peak, (8, HEAD))
        l8[at, :] = jnp.broadcast_to(total, (8, HEAD))


def pack_stats(stats, acc8, m8, l8):
    lane = lax.broadcasted_iota(jnp.int32, (SEQS, HEAD), 1)
    tail = jnp.zeros((SEQS, HEAD), F32)
    for h in range(HEADS):
        at = pl.ds(h, SEQS, stride=8)
        stats[:, h * HEAD:(h + 1) * HEAD] = acc8[at, :]
        tail = jnp.where(lane == h, m8[at, :], tail)
        tail = jnp.where(lane == HEADS + h, l8[at, :], tail)
    stats[:, HEADS * HEAD:] = tail


def put_new_rows(group, pos_ref, qkv_ref, kbuf, vbuf):
    s = lax.axis_index("sp")
    row = lax.broadcasted_iota(jnp.int32, (16, HEAD), 0)
    group_rows = pl.ds(pl.multiple_of(group * GRP, GRP), GRP)
    pairs = [[qkv_ref[group_rows, (5 * c + which) * HEAD:(5 * c + which + 1) * HEAD] for c in range(KV)]
             for which in (GROUP, GROUP + 1)]
    for j in range(GRP):
        b = group * GRP + j
        local = pos_ref[b] - s * SLOTS
        inside = jnp.where((local >= 0) & (local < SLOTS), 1, 0)
        local = jnp.clip(local, 0, SLOTS - 1)
        at = pl.ds(pl.multiple_of((local // 8) * 16, 16), 16)
        target = jnp.where(inside == 1, local % 8, 99)
        hit = (row // KV) == target
        for buf, (first, second) in zip((kbuf, vbuf), pairs):
            fresh = jnp.where(row % KV == 0, first[j:j + 1], second[j:j + 1])
            buf[b, at, :] = jnp.where(hit, fresh, buf[b, at, :].astype(F32)).astype(BF16)


def entry_kernel(pos_ref, hidden, gain, shift, b_qkv, cos, sin, w_hbm, kc_hbm, vc_hbm,
                 ko_hbm, vo_hbm, qkv, stats, cos_rows, sin_rows,
                 wbuf, kbuf, vbuf, u_s, q8, acc8, m8, l8, wsem, ksem, vsem, kosem, vosem):
    def w_copy(i):
        return pltpu.make_async_copy(w_hbm.at[0, pl.ds(i * CH, CH)], wbuf.at[pl.ds(i * CH, CH)], wsem.at[i])

    def in_copies(g):
        at = pl.ds(g * GRP, GRP)
        return (pltpu.make_async_copy(kc_hbm.at[0, at], kbuf.at[at], ksem.at[g]),
                pltpu.make_async_copy(vc_hbm.at[0, at], vbuf.at[at], vsem.at[g]))

    def out_copies(g):
        at = pl.ds(g * GRP, GRP)
        return (pltpu.make_async_copy(kbuf.at[at], ko_hbm.at[0, at], kosem.at[g]),
                pltpu.make_async_copy(vbuf.at[at], vo_hbm.at[0, at], vosem.at[g]))

    for i in range(NCH):
        w_copy(i).start()
    for g in range(NGRP):
        for copy in in_copies(g):
            copy.start()

    def pick_row(b, carry):
        p = pos_ref[b]
        cos_rows[pl.ds(b, 1), :] = cos[pl.ds(p, 1), :]
        sin_rows[pl.ds(b, 1), :] = sin[pl.ds(p, 1), :]
        return carry

    lax.fori_loop(0, SEQS, pick_row, 0)
    q8[...] = jnp.zeros_like(q8)
    u_s[...] = norm_rows(hidden[...].astype(F32), param_row(gain, 0, 0), param_row(shift, 0, 0))
    for i in range(NCH):
        w_copy(i).wait()
        piece = dot(u_s[:, i * CH:(i + 1) * CH], wbuf[i * CH:(i + 1) * CH, :])
        qkv[...] = piece + param_row(b_qkv, 0) if i == 0 else qkv[...] + piece
    turn_columns(qkv, slice(None), cos_rows[...], sin_rows[...])
    for h in range(HEADS):
        cols = (h // GROUP * 5 + h % GROUP) * HEAD
        q8[pl.ds(h, SEQS, stride=8), :] = qkv[:, cols:cols + HEAD]

    def one_group(g, carry):
        for copy in in_copies(g):
            copy.wait()
        attend(g, True, pos_ref, q8, kbuf, vbuf, acc8, m8, l8)
        put_new_rows(g, pos_ref, qkv, kbuf, vbuf)
        for copy in out_copies(g):
            copy.start()
        return carry

    lax.fori_loop(0, NGRP, one_group, 0)
    pack_stats(stats, acc8, m8, l8)

    def drain(g, carry):
        for copy in out_copies(g):
            copy.wait()
        return carry

    lax.fori_loop(0, NGRP, drain, 0)


def exit_kernel(pos_ref, qkv, hid, kc_hbm, vc_hbm, ka_hbm, va_hbm, hid_out, ko_hbm, vo_hbm,
                kbuf, vbuf, ksem, vsem, kosem, vosem):
    def in_copies(g):
        at = pl.ds(g * GRP, GRP)
        return (pltpu.make_async_copy(kc_hbm.at[1, at], kbuf.at[at], ksem.at[g]),
                pltpu.make_async_copy(vc_hbm.at[1, at], vbuf.at[at], vsem.at[g]))

    def out_copies(g):
        at = pl.ds(g * GRP, GRP)
        return (pltpu.make_async_copy(kbuf.at[at], ko_hbm.at[1, at], kosem.at[g]),
                pltpu.make_async_copy(vbuf.at[at], vo_hbm.at[1, at], vosem.at[g]))

    for g in range(NGRP):
        for copy in in_copies(g):
            copy.start()
    hid_out[...] = hid[...]

    def one_group(g, carry):
        for copy in in_copies(g):
            copy.wait()
        put_new_rows(g, pos_ref, qkv, kbuf, vbuf)
        for copy in out_copies(g):
            copy.start()
        return carry

    lax.fori_loop(0, NGRP, one_group, 0)

    def drain(g, carry):
        for copy in out_copies(g):
            copy.wait()
        return carry

    lax.fori_loop(0, NGRP, drain, 0)


def main_kernel(pos_ref, stats0, qkv0, cos_rows, sin_rows, hidden, gain, shift, b_qkv, b_dense, b_up, b_down,
                wqkv_hbm, wdense_hbm, wup_hbm, wdown_hbm, kc_hbm, vc_hbm,
                hid, qkv1_out,
                wqkv, wdense, wup, wdown, kbuf, vbuf,
                mix, part, summed, spread, x_own, x_all, o16, u16, h_s, m16, qkv1, stats1, fin, q8, acc8, m8, l8,
                w_sem, kv_sem, mix_send, mix_recv, part_send, part_recv, spread_send, spread_recv,
                q_send, q_recv, fin_send, fin_recv):
    t, s = lax.axis_index("tp"), lax.axis_index("sp")
    sends = []

    def send(src, dst, send_sem, recv_sem, axis, peer):
        copy = pltpu.make_async_remote_copy(src_ref=src, dst_ref=dst, send_sem=send_sem, recv_sem=recv_sem,
                                            device_id={axis: peer}, device_id_type=MESH)
        copy.start()
        sends.append(copy)

    def arrived(dst, send_sem, recv_sem, axis, peer):
        pltpu.make_async_remote_copy(src_ref=dst, dst_ref=dst, send_sem=send_sem, recv_sem=recv_sem,
                                     device_id={axis: peer}, device_id_type=MESH).wait_recv()

    barrier = pltpu.get_barrier_semaphore()
    for axis, me in (("tp", t), ("sp", s)):
        for d in range(1, 4):
            pl.semaphore_signal(barrier, inc=1, device_id={axis: lax.rem(me + d, 4)}, device_id_type=MESH)

    cols = [pl.ds(n * CH, CH) for n in range(NCH)]

    def dense_copy(layer, n):
        return pltpu.make_async_copy(wdense_hbm.at[layer, :, cols[n]], wdense.at[:, cols[n]], w_sem.at[0, n])

    def up_copy(layer, n):
        return pltpu.make_async_copy(wup_hbm.at[layer, cols[n]], wup.at[cols[n]], w_sem.at[1, n])

    def down_copy(layer, n):
        return pltpu.make_async_copy(wdown_hbm.at[layer, :, cols[n]], wdown.at[:, cols[n]], w_sem.at[2, n])

    def qkv_copy(n):
        return pltpu.make_async_copy(wqkv_hbm.at[1, cols[n]], wqkv.at[cols[n]], w_sem.at[3, n])

    k_copy = pltpu.make_async_copy(kc_hbm.at[1], kbuf, kv_sem.at[0])
    v_copy = pltpu.make_async_copy(vc_hbm.at[1], vbuf, kv_sem.at[1])
    for n in range(NCH):
        dense_copy(0, n).start()
    for n in range(NCH):
        up_copy(0, n).start()
    for n in range(NCH):
        down_copy(0, n).start()
    for n in range(NCH):
        qkv_copy(n).start()
    k_copy.start()
    v_copy.start()

    my_rows = pl.ds(pl.multiple_of(s * ROWS, ROWS), ROWS)
    wide = hidden[my_rows, :].astype(F32)
    for j in range(4):
        x_all[j] = wide[OWN * j:OWN * (j + 1)]
    x_own[...] = x_all[t]
    q8[...] = jnp.zeros_like(q8)
    pl.semaphore_wait(barrier, 6)

    def exchange(layer, stats):
        for d in range(1, 4):
            peer = lax.rem(s + d, 4)
            rows = pl.ds(pl.multiple_of(peer * ROWS, ROWS), ROWS)
            send(stats.at[rows], mix.at[layer, d - 1], mix_send.at[layer, d - 1], mix_recv.at[layer, d - 1], "sp", peer)

    def combine(layer, stats, qkv_rows):
        for d in range(1, 4):
            arrived(mix.at[layer, d - 1], mix_send.at[layer, d - 1], mix_recv.at[layer, d - 1], "sp", lax.rem(s + d, 4))
        shards = [stats[my_rows, :]] + [mix[layer, d] for d in range(3)]
        for h in range(HEADS):
            base = h // GROUP * 5
            q = qkv_rows[:, (base + h % GROUP) * HEAD:(base + h % GROUP + 1) * HEAD]
            k = qkv_rows[:, (base + GROUP) * HEAD:(base + GROUP + 1) * HEAD]
            v = qkv_rows[:, (base + GROUP + 1) * HEAD:(base + GROUP + 2) * HEAD]
            fresh = jnp.sum(q * k, axis=-1, keepdims=True) * (1.0 / HEAD)
            peaks = [x[:, HEADS * HEAD + h:HEADS * HEAD + h + 1] for x in shards]
            top = fresh
            for peak in peaks:
                top = jnp.maximum(top, peak)
            scale = jnp.exp(fresh - top)
            num, den = v * scale, scale
            for x, peak in zip(shards, peaks):
                scale = jnp.exp(peak - top)
                num = num + x[:, h * HEAD:(h + 1) * HEAD] * scale
                den = den + x[:, HEADS * HEAD + HEADS + h:HEADS * HEAD + HEADS + h + 1] * scale
            o16[:, h * HEAD:(h + 1) * HEAD] = (num / den).astype(BF16)

    def reduce_rows(phase, lhs, weights, layer, copy_of, reload):
        for n in range(NCH):
            copy_of(layer, n).wait()
            piece = dot(lhs[...], weights[:, n * CH:(n + 1) * CH])
            for j in range(4):
                part[phase, j, :, n * CH:(n + 1) * CH] = piece[OWN * j:OWN * (j + 1)]
            for d in range(1, 4):
                peer = lax.rem(t + d, 4)
                send(part.at[phase, peer, :, cols[n]], summed.at[phase, d - 1, :, cols[n]],
                     part_send.at[phase, d - 1, n], part_recv.at[phase, d - 1, n], "tp", peer)
            if reload:
                copy_of(layer + 1, n).start()
        for n in range(NCH):
            for d in range(1, 4):
                arrived(summed.at[phase, d - 1, :, cols[n]], part_send.at[phase, d - 1, n],
                        part_recv.at[phase, d - 1, n], "tp", lax.rem(t + d, 4))
        return part[phase, t] + summed[phase, 0] + summed[phase, 1] + summed[phase, 2]

    def spread_rows(phase, rows):
        spread[phase, t] = rows.astype(F32)
        for n in range(NCH):
            for d in range(1, 4):
                send(spread.at[phase, t, :, cols[n]], spread.at[phase, t, :, cols[n]],
                     spread_send.at[phase, d - 1, n], spread_recv.at[phase, d - 1, n], "tp", lax.rem(t + d, 4))

    def take_rows(phase, n):
        for d in range(1, 4):
            arrived(spread.at[phase, lax.rem(t - d + 4, 4), :, cols[n]], spread_send.at[phase, d - 1, n],
                    spread_recv.at[phase, d - 1, n], "tp", lax.rem(t + d, 4))
        rows = [spread[phase, j, :, n * CH:(n + 1) * CH] for j in range(4)]
        u16[...] = jnp.concatenate(rows, axis=0).astype(BF16)

    lane = lax.broadcasted_iota(jnp.int32, (ROWS, 1024), 1)
    pick = (lax.broadcasted_iota(jnp.int32, (256, 128), 0) == 2 * lax.broadcasted_iota(jnp.int32, (256, 128), 1))
    pick = jnp.where(pick, 1.0, 0.0).astype(BF16)

    def finish_layer(layer):
        last = layer == 1
        total = reduce_rows(2 * layer, o16, wdense, layer, dense_copy, not last)
        x1 = round_bf16(x_own[...] + total + param_row(b_dense, layer))
        x_own[...] = x1
        spread_rows(2 * layer, norm_rows(x1, param_row(gain, layer, 1), param_row(shift, layer, 1)))
        bias = param_row(b_up, layer)
        for n in range(NCH):
            up_copy(layer, n).wait()
            take_rows(2 * layer, n)
            for c in range(4):
                at = slice(c * 1024, (c + 1) * 1024)
                piece = dot(u16[...], wup[n * CH:(n + 1) * CH, at])
                h_s[:, at] = piece + bias[:, at] if n == 0 else h_s[:, at] + piece
            if not last:
                up_copy(layer + 1, n).start()
        for c in range(4):
            pair = h_s[:, c * 1024:(c + 1) * 1024]
            gate = jnp.minimum(pair, GELU_LIMIT)
            line = jnp.clip(pltpu.roll(pair, 1023, 1), -GELU_LIMIT, GELU_LIMIT)
            act = gate * jax.nn.sigmoid(1.702 * gate) * (line + 1.0)
            act = jnp.where(lane % 2 == 0, act, 0.0).astype(BF16)
            for k in range(4):
                at = slice(c * 512 + k * 128, c * 512 + (k + 1) * 128)
                m16[:, at] = dot(act[:, k * 256:(k + 1) * 256], pick).astype(BF16)
        total = reduce_rows(2 * layer + 1, m16, wdown, layer, down_copy, not last)
        x_own[...] = round_bf16(x_own[...] + total + param_row(b_down, layer))

    exchange(0, stats0)
    combine(0, stats0, qkv0[my_rows, :])
    finish_layer(0)

    spread_rows(1, norm_rows(x_own[...], param_row(gain, 1, 0), param_row(shift, 1, 0)))
    mine = qkv1.at[s]
    for n in range(NCH):
        qkv_copy(n).wait()
        take_rows(1, n)
        piece = dot(u16[...], wqkv[n * CH:(n + 1) * CH, :])
        mine[...] = piece + param_row(b_qkv, 1) if n == 0 else mine[...] + piece
    turn_columns(mine, slice(None), cos_rows[my_rows, :], sin_rows[my_rows, :])
    for d in range(1, 4):
        send(mine, mine, q_send.at[d - 1], q_recv.at[d - 1], "sp", lax.rem(s + d, 4))
    for d in range(1, 4):
        arrived(qkv1.at[lax.rem(s - d + 4, 4)], q_send.at[d - 1], q_recv.at[d - 1], "sp", lax.rem(s + d, 4))
    for i in range(4):
        for h in range(HEADS):
            at = (h // GROUP * 5 + h % GROUP) * HEAD
            q8[pl.ds(i * ROWS * 8 + h, ROWS, stride=8), :] = qkv1[i, :, at:at + HEAD]
        qkv1_out[i * ROWS:(i + 1) * ROWS, :] = qkv1[i]
    k_copy.wait()
    v_copy.wait()

    def one_group(g, carry):
        attend(g, False, pos_ref, q8, kbuf, vbuf, acc8, m8, l8)
        return carry

    lax.fori_loop(0, NGRP, one_group, 0)
    pack_stats(stats1, acc8, m8, l8)
    exchange(1, stats1)
    combine(1, stats1, qkv1[s])
    finish_layer(1)

    twin = s + 1 - 2 * lax.rem(s, 2)
    across = lax.rem(s + 2, 4)
    fin[s, t] = x_own[...]

    def forward(block, kind, index, axis, peer):
        send(block, block, fin_send.at[kind, index], fin_recv.at[kind, index], axis, peer)

    def landed(block, kind, index, axis, peer):
        arrived(block, fin_send.at[kind, index], fin_recv.at[kind, index], axis, peer)

    for d in range(1, 4):
        forward(fin.at[s, t], 0, d, "tp", lax.rem(t + d, 4))
    forward(fin.at[s, t], 1, 0, "sp", across)
    forward(fin.at[s, t], 2, 0, "sp", twin)
    for d in range(1, 4):
        block = fin.at[s, lax.rem(t - d + 4, 4)]
        landed(block, 0, d, "tp", lax.rem(t + d, 4))
        forward(block, 1, d, "sp", across)
        forward(block, 2, d, "sp", twin)
    for d in range(4):
        block = fin.at[across, lax.rem(t - d + 4, 4)]
        landed(block, 1, d, "sp", across)
        forward(block, 3, d, "sp", twin)
    diagonal = lax.rem(twin + 2, 4)
    for d in range(4):
        landed(fin.at[twin, lax.rem(t - d + 4, 4)], 2, d, "sp", twin)
        landed(fin.at[diagonal, lax.rem(t - d + 4, 4)], 3, d, "sp", twin)
    for i in range(4):
        rows = jnp.concatenate([fin[i, j] for j in range(4)], axis=0)
        hid[i * ROWS:(i + 1) * ROWS, :] = rows.astype(BF16)
    for copy in sends:
        copy.wait_send()


def solution(mesh):
    cache_spec = P(None, "dp", "sp", "tp", None)
    in_specs = (P("dp", None), P("dp"), cache_spec, cache_spec, P(), P(), P(None, None, "tp"), P(None, "tp"),
                P(None, "tp", None), P(), P(None, None, "tp"), P(None, "tp"), P(None, "tp", None), P())
    out_specs = (P("dp", None), cache_spec, cache_spec)
    cos_np, sin_np = rope_tables()
    vmem, smem, hbm = (pl.BlockSpec(memory_space=m) for m in (pltpu.VMEM, pltpu.SMEM, pl.ANY))
    dma = pltpu.SemaphoreType.DMA

    def device_step(hidden, positions, k_cache, v_cache, ln_gain, ln_bias, w_qkv, b_qkv, w_dense, b_dense,
                    w_up, b_up, w_down, b_down):
        flat = (2, SEQS, SLOTS * KV, HEAD)
        kc, vc = k_cache.reshape(flat), v_cache.reshape(flat)
        cache = jax.ShapeDtypeStruct(flat, BF16)
        kv_buffers = [pltpu.VMEM(flat[1:], BF16)] * 2
        row8 = [pltpu.VMEM((SEQS * 8, HEAD), F32)] * 4
        ko, vo, qkv0, stats0, cos_rows, sin_rows = pl.pallas_call(
            entry_kernel,
            out_shape=(cache, cache, jax.ShapeDtypeStruct((SEQS, QKV), F32), jax.ShapeDtypeStruct((SEQS, STAT), F32),
                       jax.ShapeDtypeStruct((SEQS, HEAD), F32), jax.ShapeDtypeStruct((SEQS, HEAD), F32)),
            in_specs=[smem] + [vmem] * 6 + [hbm] * 3,
            out_specs=(hbm, hbm, vmem, vmem, vmem, vmem),
            scratch_shapes=[pltpu.VMEM((D, QKV), BF16)] + kv_buffers + [pltpu.VMEM((SEQS, D), BF16)] + row8
            + [dma((NCH,))] + [dma((NGRP,))] * 4,
            compiler_params=pltpu.CompilerParams(vmem_limit_bytes=VMEM_MAX),
            name="entry",
        )(positions, hidden, ln_gain, ln_bias, b_qkv, cos_np, sin_np, w_qkv, kc, vc)

        hid, qkv1 = pl.pallas_call(
            main_kernel,
            out_shape=(jax.ShapeDtypeStruct((SEQS, D), BF16), jax.ShapeDtypeStruct((SEQS, QKV), F32)),
            in_specs=[smem] + [vmem] * 11 + [hbm] * 6,
            out_specs=(vmem, vmem),
            scratch_shapes=[
                pltpu.VMEM((D, QKV), BF16), pltpu.VMEM((HEADS * HEAD, D), BF16), pltpu.VMEM((D, UP), BF16),
                pltpu.VMEM((FF, D), BF16)] + kv_buffers + [
                pltpu.VMEM((2, 3, ROWS, STAT), F32),
                pltpu.VMEM((4, 4, OWN, D), F32),
                pltpu.VMEM((4, 3, OWN, D), F32),
                pltpu.VMEM((3, 4, OWN, D), F32),
                pltpu.VMEM((OWN, D), F32),
                pltpu.VMEM((4, OWN, D), F32),
                pltpu.VMEM((ROWS, HEADS * HEAD), BF16),
                pltpu.VMEM((ROWS, CH), BF16),
                pltpu.VMEM((ROWS, UP), F32),
                pltpu.VMEM((ROWS, FF), BF16),
                pltpu.VMEM((4, ROWS, QKV), F32),
                pltpu.VMEM((SEQS, STAT), F32),
                pltpu.VMEM((4, 4, OWN, D), F32),
            ] + row8 + [
                dma((4, NCH)), dma((2,)), dma((2, 3)), dma((2, 3)), dma((4, 3, NCH)), dma((4, 3, NCH)),
                dma((3, 3, NCH)), dma((3, 3, NCH)), dma((3,)), dma((3,)), dma((4, 4)), dma((4, 4))],
            compiler_params=pltpu.CompilerParams(vmem_limit_bytes=VMEM_MAX, collective_id=0, has_side_effects=True),
            name="main",
        )(positions, stats0, qkv0, cos_rows, sin_rows, hidden, ln_gain, ln_bias, b_qkv, b_dense, b_up, b_down,
          w_qkv, w_dense, w_up, w_down, kc, vc)

        hidden_out, ko, vo = pl.pallas_call(
            exit_kernel,
            out_shape=(jax.ShapeDtypeStruct((SEQS, D), BF16), cache, cache),
            in_specs=[smem, vmem, vmem] + [hbm] * 4,
            out_specs=(vmem, hbm, hbm),
            scratch_shapes=kv_buffers + [dma((NGRP,))] * 4,
            input_output_aliases={5: 1, 6: 2},
            compiler_params=pltpu.CompilerParams(vmem_limit_bytes=VMEM_MAX),
            name="exit",
        )(positions, qkv1, hid, kc, vc, ko, vo)
        return hidden_out, ko.reshape(k_cache.shape), vo.reshape(v_cache.shape)

    return jax.shard_map(device_step, mesh=mesh, in_specs=in_specs, out_specs=out_specs, check_vma=False)
```

profile of v0, /device:TPU:1, one launch (start us, length us, event | category | flops | bytes accessed | tf_op | source)
XLA Modules:
  0.0 128.8 jit_solution(2650781965146984525)
XLA Ops:
  0.6 24.6 %entry.1 = (bf16[2,64,256,128]{3,2,1,0:T(8,128)(2,1)}, bf16[2,64,256,128]{3,2,1,0:T(8,128)(2,1)}, f32[64,1280]{1,0:T(8,128)}, f32[64,896]{1,0:T(8,128)}, f32[64,128]{1,0:T(8,128)}, /*index=5*/f32[64,128]{1,0:T(8,128)}) custom-call(s32[64]{0:T(128)} %pos_ref.5, bf16[64,3072]{1,0:T(8,128)(2,1)} %hidden.3, bf16[2,2,3072]{2,1,0:T(2,128)(2,1)} %gain.3, ...), custom_call_target="tpu_custom_call" | custom-call | tf_op jit(solution)/shard_map/entry/pallas_call | solution.py:469
  25.2 94.9 %main.1 = (bf16[64,3072]{1,0:T(8,128)(2,1)}, f32[64,1280]{1,0:T(8,128)}) custom-call(s32[64]{0:T(128)} %pos_ref.5, f32[64,896]{1,0:T(8,128)} %get-tuple-element.14.stats0, f32[64,1280]{1,0:T(8,128)} %get-tuple-element.15.qkv0, f32[64,128]{1,0:T(8,128)} %get-tuple-element.16.cos_rows, f32[64,128]{1,0:T(8,128)} %get-tuple-element.17.sin_rows, ...), custom_call_target="tpu_custom_call" | custom-call | tf_op jit(solution)/shard_map/main/pallas_call | solution.py:481
  120.2 8.4 %exit.1 = (bf16[64,3072]{1,0:T(8,128)(2,1)}, bf16[2,64,256,128]{3,2,1,0:T(8,128)(2,1)}, bf16[2,64,256,128]{3,2,1,0:T(8,128)(2,1)}) custom-call(s32[64]{0:T(128)} %pos_ref.5, f32[64,1280]{1,0:T(8,128)} %get-tuple-element.18.qkv, bf16[64,3072]{1,0:T(8,128)(2,1)} %get-tuple-element.19.hid, ...), custom_call_target="tpu_custom_call", output_to_operand_aliasing={{1}: (5, {}), {2}: (6, {})} | custom-call | tf_op jit(solution)/shard_map/exit/pallas_call | solution.py:510
where the time goes:
time: 129 us
  Pallas kernels  128 us (99%)
    pallas_call x1, Pallas kernels, device_step(): pl.pallas_call(main_kernel, out_shape=(jax.ShapeDtypeStruct((SEQS, D), BF...  94.9 us
    pallas_call x1, Pallas kernels, device_step(): pl.pallas_call(entry_kernel, out_shape=(cache, cache, jax.ShapeDtypeStruc...  24.6 us
    pallas_call x1, Pallas kernels, device_step(): pl.pallas_call(exit_kernel, out_shape=(jax.ShapeDtypeStruct((SEQS, D), BF...  8.44 us

commit v1 on v0

--- a/solution.py
+++ b/solution.py
@@ -79,30 +79,33 @@
             ref[rows, cols] = round_bf16(x)
 
 
-def attend(group, sparse, pos_ref, q8, kbuf, vbuf, acc8, m8, l8):
+def attend(sparse, pos_ref, q8, kbuf, vbuf, s8, acc8, m8, l8):
     t, s = lax.axis_index("tp"), lax.axis_index("sp")
-    row = lax.broadcasted_iota(jnp.int32, (8, 2 * SLOTS), 0)
-    col = lax.broadcasted_iota(jnp.int32, (8, 2 * SLOTS), 1)
+    row = lax.broadcasted_iota(jnp.int32, (8, KV * SLOTS), 0)
+    col = lax.broadcasted_iota(jnp.int32, (8, KV * SLOTS), 1)
     slot = s * SLOTS + col // KV
     same = (col % KV) == row // GROUP
     vertical = (slot // BLOCK_SIZE + (t * HEADS + row) + 1) % VERT_STRIDE == 0
-    for j in range(GRP):
-        b = group * GRP + j
+    for b in range(SEQS):
+        at = slice(b * 8, b * 8 + 8)
         p = pos_ref[b]
-        at = pl.ds(pl.multiple_of(b * 8, 8), 8)
         scores = lax.dot_general(q8[at, :].astype(BF16), kbuf[b], (((1,), (1,)), ((), ())), preferred_element_type=F32)
-        scores = scores * (1.0 / HEAD)
         keep = (slot < p) & same
         if sparse:
             near = (p // BLOCK_SIZE - slot // BLOCK_SIZE) < LOCAL_BLOCKS
             keep = keep & (near | vertical)
-        scores = jnp.where(keep, scores, MASKED)
-        peak = jnp.max(scores, axis=-1, keepdims=True)
-        weights = jnp.where(keep, jnp.exp(scores - peak), 0.0)
-        total = jnp.sum(weights, axis=-1, keepdims=True)
-        acc8[at, :] = dot(weights.astype(BF16), vbuf[b])
-        m8[at, :] = jnp.broadcast_to(peak, (8, HEAD))
-        l8[at, :] = jnp.broadcast_to(total, (8, HEAD))
+        s8[at, :] = jnp.where(keep, scores * (1.0 / HEAD), -jnp.inf)
+    for r in range(8):
+        at = slice(r * SEQS, (r + 1) * SEQS)
+        scores = s8[at, :]
+        peak = jnp.maximum(jnp.max(scores, axis=-1, keepdims=True), MASKED)
+        weights = jnp.exp(scores - peak)
+        s8[at, :] = weights
+        m8[at, :] = jnp.broadcast_to(peak, (SEQS, HEAD))
+        l8[at, :] = jnp.broadcast_to(jnp.sum(weights, axis=-1, keepdims=True), (SEQS, HEAD))
+    for b in range(SEQS):
+        at = slice(b * 8, b * 8 + 8)
+        acc8[at, :] = dot(s8[at, :].astype(BF16), vbuf[b])
 
 
 def pack_stats(stats, acc8, m8, l8):
@@ -137,7 +140,7 @@
 
 def entry_kernel(pos_ref, hidden, gain, shift, b_qkv, cos, sin, w_hbm, kc_hbm, vc_hbm,
                  ko_hbm, vo_hbm, qkv, stats, cos_rows, sin_rows,
-                 wbuf, kbuf, vbuf, u_s, q8, acc8, m8, l8, wsem, ksem, vsem, kosem, vosem):
+                 wbuf, kbuf, vbuf, u_s, q8, s8, acc8, m8, l8, wsem, ksem, vsem, kosem, vosem):
     def w_copy(i):
         return pltpu.make_async_copy(w_hbm.at[0, pl.ds(i * CH, CH)], wbuf.at[pl.ds(i * CH, CH)], wsem.at[i])
 
@@ -178,13 +181,13 @@
     def one_group(g, carry):
         for copy in in_copies(g):
             copy.wait()
-        attend(g, True, pos_ref, q8, kbuf, vbuf, acc8, m8, l8)
         put_new_rows(g, pos_ref, qkv, kbuf, vbuf)
         for copy in out_copies(g):
             copy.start()
         return carry
 
     lax.fori_loop(0, NGRP, one_group, 0)
+    attend(True, pos_ref, q8, kbuf, vbuf, s8, acc8, m8, l8)
     pack_stats(stats, acc8, m8, l8)
 
     def drain(g, carry):
@@ -234,7 +237,7 @@
                 wqkv_hbm, wdense_hbm, wup_hbm, wdown_hbm, kc_hbm, vc_hbm,
                 hid, qkv1_out,
                 wqkv, wdense, wup, wdown, kbuf, vbuf,
-                mix, part, summed, spread, x_own, x_all, o16, u16, h_s, m16, qkv1, stats1, fin, q8, acc8, m8, l8,
+                mix, part, summed, spread, x_own, x_all, o16, u16, h_s, m16, qkv1, stats1, fin, q8, s8, acc8, m8, l8,
                 w_sem, kv_sem, mix_send, mix_recv, part_send, part_recv, spread_send, spread_recv,
                 q_send, q_recv, fin_send, fin_recv):
     t, s = lax.axis_index("tp"), lax.axis_index("sp")
@@ -406,11 +409,7 @@
     k_copy.wait()
     v_copy.wait()
 
-    def one_group(g, carry):
-        attend(g, False, pos_ref, q8, kbuf, vbuf, acc8, m8, l8)
-        return carry
-
-    lax.fori_loop(0, NGRP, one_group, 0)
+    attend(False, pos_ref, q8, kbuf, vbuf, s8, acc8, m8, l8)
     pack_stats(stats1, acc8, m8, l8)
     exchange(1, stats1)
     combine(1, stats1, qkv1[s])
@@ -465,7 +464,7 @@
         kc, vc = k_cache.reshape(flat), v_cache.reshape(flat)
         cache = jax.ShapeDtypeStruct(flat, BF16)
         kv_buffers = [pltpu.VMEM(flat[1:], BF16)] * 2
-        row8 = [pltpu.VMEM((SEQS * 8, HEAD), F32)] * 4
+        row8 = [pltpu.VMEM((SEQS * 8, n * HEAD), F32) for n in (1, 2, 1, 1, 1)]
         ko, vo, qkv0, stats0, cos_rows, sin_rows = pl.pallas_call(
             entry_kernel,
             out_shape=(cache, cache, jax.ShapeDtypeStruct((SEQS, QKV), F32), jax.ShapeDtypeStruct((SEQS, STAT), F32),

time: 129 us -> 102 us (0.79)
  Pallas kernels: 128 us -> 101 us
    pallas_call x1, Pallas kernels: 94.9 us -> 80.8 us  [device_step(): pl.pallas_call(main_kernel, out_shape=(jax.ShapeDtypeStruct((SEQS, D), BF...]
    pallas_call x1, Pallas kernels: 24.6 us -> 11.8 us  [device_step(): pl.pallas_call(entry_kernel, out_shape=(cache, cache, jax.ShapeDtypeStruc...]
where the time goes in v1:
time: 102 us
  Pallas kernels  101 us (99%)
    pallas_call x1, Pallas kernels, device_step(): pl.pallas_call(main_kernel, out_shape=(jax.ShapeDtypeStruct((SEQS, D), BF...  80.8 us
    pallas_call x1, Pallas kernels, device_step(): pl.pallas_call(entry_kernel, out_shape=(cache, cache, jax.ShapeDtypeStruc...  11.8 us
    pallas_call x1, Pallas kernels, device_step(): pl.pallas_call(exit_kernel, out_shape=(jax.ShapeDtypeStruct((SEQS, D), BF...  8.44 us

profile of v1, /device:TPU:1, one launch (start us, length us, event | category | flops | bytes accessed | tf_op | source)
XLA Modules:
  0.0 101.9 jit_solution(4386210923631265870)
XLA Ops:
  0.6 11.8 %entry.1 = (bf16[2,64,256,128]{3,2,1,0:T(8,128)(2,1)}, bf16[2,64,256,128]{3,2,1,0:T(8,128)(2,1)}, f32[64,1280]{1,0:T(8,128)}, f32[64,896]{1,0:T(8,128)}, f32[64,128]{1,0:T(8,128)}, /*index=5*/f32[64,128]{1,0:T(8,128)}) custom-call(s32[64]{0:T(128)} %pos_ref.5, bf16[64,3072]{1,0:T(8,128)(2,1)} %hidden.3, bf16[2,2,3072]{2,1,0:T(2,128)(2,1)} %gain.3, ...), custom_call_target="tpu_custom_call" | custom-call | tf_op jit(solution)/shard_map/entry/pallas_call | solution.py:468
  12.4 80.8 %main.1 = (bf16[64,3072]{1,0:T(8,128)(2,1)}, f32[64,1280]{1,0:T(8,128)}) custom-call(s32[64]{0:T(128)} %pos_ref.5, f32[64,896]{1,0:T(8,128)} %get-tuple-element.14.stats0, f32[64,1280]{1,0:T(8,128)} %get-tuple-element.15.qkv0, f32[64,128]{1,0:T(8,128)} %get-tuple-element.16.cos_rows, f32[64,128]{1,0:T(8,128)} %get-tuple-element.17.sin_rows, ...), custom_call_target="tpu_custom_call" | custom-call | tf_op jit(solution)/shard_map/main/pallas_call | solution.py:480
  93.2 8.4 %exit.1 = (bf16[64,3072]{1,0:T(8,128)(2,1)}, bf16[2,64,256,128]{3,2,1,0:T(8,128)(2,1)}, bf16[2,64,256,128]{3,2,1,0:T(8,128)(2,1)}) custom-call(s32[64]{0:T(128)} %pos_ref.5, f32[64,1280]{1,0:T(8,128)} %get-tuple-element.18.qkv, bf16[64,3072]{1,0:T(8,128)(2,1)} %get-tuple-element.19.hid, ...), custom_call_target="tpu_custom_call", output_to_operand_aliasing={{1}: (5, {}), {2}: (6, {})} | custom-call | tf_op jit(solution)/shard_map/exit/pallas_call | solution.py:509

commit v2 on v1

v2 whole, which is shorter than its diff:
```python
import functools

import jax
import jax.numpy as jnp
import numpy as np
from jax import lax
from jax.experimental import pallas as pl
from jax.experimental.pallas import tpu as pltpu
from jax.sharding import PartitionSpec as P

MESH = pl.DeviceIdType.MESH
F32 = jnp.float32
BF16 = jnp.bfloat16
BLOCK_SIZE = 64
LOCAL_BLOCKS = 16
VERT_STRIDE = 8
ROPE_THETA = 1000000.0
GELU_LIMIT = 20.0
NORM_EPS = 0.00001
MASKED = -1e30

SEQS = 64
ROWS = 16
OWN = 8
SEQ_LEN = 512
SLOTS = 128
D = 3072
HEAD = 128
KV = 2
GROUP = 3
HEADS = KV * GROUP
QKV = 1280
QW = HEADS * HEAD
KVW = 2 * KV * HEAD
UP = 4096
FF = 2048
STAT = HEADS * HEAD + HEAD
NCH = 3
CH = D // NCH
GRP = 8
NGRP = SEQS // GRP
VMEM_MAX = 67043328


def rope_table():
    half = HEAD // 2
    inv = (ROPE_THETA ** (-np.arange(half).astype(np.float32) * np.float32(2.0 / HEAD))).astype(np.float32)
    angle = (np.arange(SEQ_LEN).astype(np.float32)[:, None] * inv[None, :]).astype(np.float64)
    cos, sin = np.cos(angle).astype(np.float32), np.sin(angle).astype(np.float32)
    return np.concatenate([cos, sin], 1)


def norm_rows(wide, gain, shift):
    mean = jnp.mean(wide, axis=-1, keepdims=True)
    centred = wide - mean
    var = jnp.mean(centred * centred, axis=-1, keepdims=True)
    return (centred * lax.rsqrt(var + NORM_EPS) * gain + shift).astype(BF16)


def param_row(ref, layer, which=None):
    rows = ref[...] if which is None else ref[layer]
    pick = layer if which is None else which
    return rows.astype(F32)[pick:pick + 1]


def round_bf16(x):
    return x.astype(BF16).astype(F32)


def dot(a, b):
    return jnp.dot(a, b, preferred_element_type=F32)


def turn_columns(acc, q_ref, kv_ref, cos, sin):
    for c in range(KV):
        for g in range(GROUP + 2):
            x = acc[:, (c * 5 + g) * HEAD:(c * 5 + g + 1) * HEAD]
            if g <= GROUP:
                x = x * cos + pltpu.roll(x, HEAD // 2, 1) * sin
            x = round_bf16(x)
            if g < GROUP:
                q_ref[:, (c * GROUP + g) * HEAD:(c * GROUP + g + 1) * HEAD] = x
            else:
                at = (c * 2 + g - GROUP) * HEAD
                kv_ref[:, at:at + HEAD] = x


def attend(sparse, pos_ref, q8, kbuf, vbuf, s8, acc8, ml8):
    t, s = lax.axis_index("tp"), lax.axis_index("sp")
    row = lax.broadcasted_iota(jnp.int32, (8, KV * SLOTS), 0)
    col = lax.broadcasted_iota(jnp.int32, (8, KV * SLOTS), 1)
    slot = s * SLOTS + col // KV
    same = (col % KV) == row // GROUP
    vertical = (slot // BLOCK_SIZE + (t * HEADS + row) + 1) % VERT_STRIDE == 0
    for b in range(SEQS):
        at = slice(b * 8, b * 8 + 8)
        p = pos_ref[b]
        scores = lax.dot_general(q8[at, :].astype(BF16), kbuf[b], (((1,), (1,)), ((), ())), preferred_element_type=F32)
        keep = (slot < p) & same
        if sparse:
            near = (p // BLOCK_SIZE - slot // BLOCK_SIZE) < LOCAL_BLOCKS
            keep = keep & (near | vertical)
        s8[at, :] = jnp.where(keep, scores * (1.0 / HEAD), -jnp.inf)
    for r in range(8):
        at = slice(r * SEQS, (r + 1) * SEQS)
        scores = s8[at, :]
        peak = jnp.maximum(jnp.max(scores, axis=-1, keepdims=True), MASKED)
        weights = jnp.exp(scores - peak)
        s8[at, :] = weights
        total = jnp.sum(weights, axis=-1, keepdims=True)
        low = lax.broadcasted_iota(jnp.int32, (SEQS, HEAD), 1) < HEADS
        ml8[at, :] = jnp.where(low, peak, total)
    for b in range(SEQS):
        at = slice(b * 8, b * 8 + 8)
        acc8[at, :] = dot(s8[at, :].astype(BF16), vbuf[b])


def pack_stats(stats, acc8, ml8):
    lane = lax.broadcasted_iota(jnp.int32, (SEQS, HEAD), 1)
    tail = jnp.zeros((SEQS, HEAD), F32)
    for h in range(HEADS):
        at = pl.ds(h, SEQS, stride=8)
        stats[:, h * HEAD:(h + 1) * HEAD] = acc8[at, :]
        tail = jnp.where((lane == h) | (lane == HEADS + h), ml8[at, :], tail)
    stats[:, HEADS * HEAD:] = tail


def put_new_rows(group, pos_ref, kv_ref, kbuf, vbuf):
    s = lax.axis_index("sp")
    row = lax.broadcasted_iota(jnp.int32, (16, HEAD), 0)
    fresh_rows = kv_ref[pl.ds(pl.multiple_of(group * GRP, GRP), GRP), :]
    for j in range(GRP):
        b = group * GRP + j
        local = pos_ref[b] - s * SLOTS
        inside = jnp.where((local >= 0) & (local < SLOTS), 1, 0)
        local = jnp.clip(local, 0, SLOTS - 1)
        at = pl.ds(pl.multiple_of((local // 8) * 16, 16), 16)
        target = jnp.where(inside == 1, local % 8, 99)
        hit = (row // KV) == target
        for i, buf in enumerate((kbuf, vbuf)):
            first, second = (fresh_rows[j:j + 1, (2 * c + i) * HEAD:(2 * c + i + 1) * HEAD] for c in range(KV))
            fresh = jnp.where(row % KV == 0, first, second)
            buf[b, at, :] = jnp.where(hit, fresh, buf[b, at, :].astype(F32)).astype(BF16)


def exit_kernel(pos_ref, kv0, kv1, hid, kc_hbm, vc_hbm, hid_out, ko_hbm, vo_hbm, kbuf, vbuf, sems):
    def copies(layer, g, out):
        at = pl.ds(g * GRP, GRP)
        pairs = ((kc_hbm, kbuf, ko_hbm), (vc_hbm, vbuf, vo_hbm))
        return [pltpu.make_async_copy(buf.at[layer, at] if out else src.at[layer, at],
                                      dst.at[layer, at] if out else buf.at[layer, at], sems.at[i + 2 * out, layer, g])
                for i, (src, buf, dst) in enumerate(pairs)]

    for layer in range(2):
        for g in range(NGRP):
            for copy in copies(layer, g, 0):
                copy.start()
    hid_out[...] = hid[...]
    for layer, kv in enumerate((kv0, kv1)):
        def one_group(g, carry, layer=layer, kv=kv):
            for copy in copies(layer, g, 0):
                copy.wait()
            put_new_rows(g, pos_ref, kv, kbuf.at[layer], vbuf.at[layer])
            for copy in copies(layer, g, 1):
                copy.start()
            return carry

        lax.fori_loop(0, NGRP, one_group, 0)
    for layer in range(2):
        def drain(g, carry, layer=layer):
            for copy in copies(layer, g, 1):
                copy.wait()
            return carry

        lax.fori_loop(0, NGRP, drain, 0)


def main_kernel(pos_ref, hidden, gain, shift, b_qkv, b_dense, b_up, b_down, table,
                wqkv_hbm, wdense_hbm, wup_hbm, wdown_hbm, kc_hbm, vc_hbm,
                hid, kv0, kv1_out,
                wqkv, wdense, wup, wdown, kbuf, vbuf,
                mix, part, summed, spread, x_own, o16, u16, h_s, m16, u_s, acc, q0, q1, kv1, stats0, stats1, fin,
                cos_rows, sin_rows, q8, s8, acc8, ml8,
                w_sem, kv_sem, mix_send, mix_recv, part_send, part_recv, spread_send, spread_recv,
                q_send, q_recv, fin_send, fin_recv, z_send):
    t, s = lax.axis_index("tp"), lax.axis_index("sp")
    owner = (t == 1) | (t == 2)
    half = jnp.clip(t - 1, 0, 1)
    unsent = {}

    def remote(src, dst, send_sem, recv_sem, axis, peer):
        return pltpu.make_async_remote_copy(src_ref=src, dst_ref=dst, send_sem=send_sem, recv_sem=recv_sem,
                                            device_id={axis: peer}, device_id_type=MESH)

    def send(*args, when=None, key=None):
        def go():
            remote(*args).start()

        def done():
            remote(*args).wait_send()

        if when is None:
            go()
        else:
            pl.when(when)(go)
        unsent.setdefault(key, []).append((done, when))

    def flush(key):
        for done, when in unsent.pop(key):
            if when is None:
                done()
            else:
                pl.when(when)(done)

    def arrived(*args):
        remote(*args).wait_recv()

    barrier = pltpu.get_barrier_semaphore()
    for axis, me in (("tp", t), ("sp", s)):
        for d in range(1, 4):
            pl.semaphore_signal(barrier, inc=1, device_id={axis: lax.rem(me + d, 4)}, device_id_type=MESH)

    cols = [pl.ds(n * CH, CH) for n in range(NCH)]

    def dense_copy(layer, n):
        return pltpu.make_async_copy(wdense_hbm.at[layer, :, cols[n]], wdense.at[:, cols[n]], w_sem.at[0, n])

    def up_copy(layer, n):
        return pltpu.make_async_copy(wup_hbm.at[layer, cols[n]], wup.at[cols[n]], w_sem.at[1, n])

    def down_copy(layer, n):
        return pltpu.make_async_copy(wdown_hbm.at[layer, :, cols[n]], wdown.at[:, cols[n]], w_sem.at[2, n])

    def qkv_copy(layer, n):
        return pltpu.make_async_copy(wqkv_hbm.at[layer, cols[n]], wqkv.at[cols[n]], w_sem.at[3, n])

    def k_copy(layer):
        return pltpu.make_async_copy(kc_hbm.at[layer], kbuf, kv_sem.at[0])

    def v_copy(layer):
        return pltpu.make_async_copy(vc_hbm.at[layer], vbuf, kv_sem.at[1])

    for n in range(NCH):
        qkv_copy(0, n).start()
    k_copy(0).start()
    v_copy(0).start()
    for copy_of in (dense_copy, up_copy, down_copy):
        for n in range(NCH):
            copy_of(0, n).start()

    my_rows = pl.ds(pl.multiple_of(s * ROWS, ROWS), ROWS)

    def pick_row(b, carry):
        p = pos_ref[b]
        cos_rows[pl.ds(b, 1), :] = table[pl.ds(p, 1), :]
        return carry

    lax.fori_loop(0, SEQS, pick_row, 0)
    both = cos_rows[...]
    other = pltpu.roll(both, HEAD // 2, 1)
    low = lax.broadcasted_iota(jnp.int32, (SEQS, HEAD), 1) < HEAD // 2
    cos_rows[...] = jnp.where(low, both, other)
    sin_rows[...] = jnp.where(low, -other, both)
    q8[...] = jnp.zeros_like(q8)
    u_s[...] = norm_rows(hidden[...].astype(F32), param_row(gain, 0, 0), param_row(shift, 0, 0))
    wide = hidden[my_rows, :].astype(F32)
    x_own[...] = jnp.where(half == 0, wide[:OWN], wide[OWN:])
    for n in range(NCH):
        qkv_copy(0, n).wait()
        piece = dot(u_s[:, n * CH:(n + 1) * CH], wqkv[n * CH:(n + 1) * CH, :])
        acc[...] = piece + param_row(b_qkv, 0) if n == 0 else acc[...] + piece
        qkv_copy(1, n).start()
    turn_columns(acc, q0, kv0, cos_rows[...], sin_rows[...])
    for h in range(HEADS):
        q8[pl.ds(h, SEQS, stride=8), :] = q0[:, h * HEAD:(h + 1) * HEAD]
    k_copy(0).wait()
    v_copy(0).wait()
    attend(True, pos_ref, q8, kbuf, vbuf, s8, acc8, ml8)
    k_copy(1).start()
    v_copy(1).start()
    pack_stats(stats0, acc8, ml8)
    pl.semaphore_wait(barrier, 6)

    def exchange(layer, stats):
        for d in (2, 1, 3):
            peer = lax.rem(s + d, 4)
            rows = pl.ds(pl.multiple_of(peer * ROWS, ROWS), ROWS)
            send(stats.at[rows], mix.at[layer, d - 1], mix_send.at[layer, d - 1], mix_recv.at[layer, d - 1], "sp", peer)

    def combine(layer, stats, q_rows, kv_rows):
        for d in range(1, 4):
            arrived(mix.at[layer, d - 1], mix.at[layer, d - 1], mix_send.at[layer, d - 1], mix_recv.at[layer, d - 1],
                    "sp", lax.rem(s + d, 4))
        shards = [stats[my_rows, :]] + [mix[layer, d] for d in range(3)]
        for h in range(HEADS):
            c = h // GROUP
            q = q_rows[:, h * HEAD:(h + 1) * HEAD]
            k = kv_rows[:, 2 * c * HEAD:(2 * c + 1) * HEAD]
            v = kv_rows[:, (2 * c + 1) * HEAD:(2 * c + 2) * HEAD]
            fresh = jnp.sum(q * k, axis=-1, keepdims=True) * (1.0 / HEAD)
            peaks = [x[:, QW + h:QW + h + 1] for x in shards]
            top = fresh
            for peak in peaks:
                top = jnp.maximum(top, peak)
            scale = jnp.exp(fresh - top)
            num, den = v * scale, scale
            for x, peak in zip(shards, peaks):
                scale = jnp.exp(peak - top)
                num = num + x[:, h * HEAD:(h + 1) * HEAD] * scale
                den = den + x[:, QW + HEADS + h:QW + HEADS + h + 1] * scale
            o16[:, h * HEAD:(h + 1) * HEAD] = (num / den).astype(BF16)

    def reduce_rows(phase, lhs, weights, layer, copy_of, reload):
        turn = phase % 2
        if phase >= 2:
            flush(("part", phase - 2))
        for n in range(NCH):
            copy_of(layer, n).wait()
            piece = dot(lhs[...], weights[:, n * CH:(n + 1) * CH])
            for i in range(2):
                part[turn, i, :, n * CH:(n + 1) * CH] = piece[OWN * i:OWN * (i + 1)]
                slot = jnp.clip(lax.rem(t - (i + 1) + 4, 4) - 1, 0, 2)
                send(part.at[turn, i, :, cols[n]], summed.at[turn, slot, :, cols[n]],
                     part_send.at[phase, i, n], part_recv.at[phase, slot, n], "tp", i + 1, when=t != i + 1,
                     key=("part", phase))
            if reload:
                copy_of(layer + 1, n).start()

    def sum_rows(phase, n):
        turn = phase % 2
        for d in range(3):
            dst = summed.at[turn, d, :, cols[n]]
            arrived(dst, dst, part_send.at[phase, 0, n], part_recv.at[phase, d, n], "tp", lax.rem(t + 1, 4))
        at = slice(n * CH, (n + 1) * CH)
        return part[turn, half, :, at] + summed[turn, 0, :, at] + summed[turn, 1, :, at] + summed[turn, 2, :, at]

    def add_rows(phase, bias):
        for n in range(NCH):
            at = slice(n * CH, (n + 1) * CH)
            x_own[:, at] = round_bf16(x_own[:, at] + sum_rows(phase, n) + bias[:, at])

    def spread_rows(phase, layer, which):
        rows = norm_rows(x_own[...], param_row(gain, layer, which), param_row(shift, layer, which))
        spread[phase % 2, half] = rows.astype(F32)

    def send_rows(phase):
        for n in range(NCH):
            for d in range(1, 4):
                block = spread.at[phase % 2, half, :, cols[n]]
                send(block, block, spread_send.at[phase, d - 1, n], spread_recv.at[phase, half, n], "tp",
                     lax.rem(t + d, 4), when=owner, key=("spread", phase))

    def take_rows(phase, n):
        for i in range(2):
            @pl.when(t != i + 1)
            def _():
                dst = spread.at[phase % 2, i, :, cols[n]]
                arrived(dst, dst, spread_send.at[phase, 0, n], spread_recv.at[phase, i, n], "tp", lax.rem(t + 1, 4))
        at = slice(n * CH, (n + 1) * CH)
        u16[...] = jnp.concatenate([spread[phase % 2, 0, :, at], spread[phase % 2, 1, :, at]], axis=0).astype(BF16)

    lane = lax.broadcasted_iota(jnp.int32, (ROWS, 1024), 1)
    pick = (lax.broadcasted_iota(jnp.int32, (256, 128), 0) == 2 * lax.broadcasted_iota(jnp.int32, (256, 128), 1))
    pick = jnp.where(pick, 1.0, 0.0).astype(BF16)

    def finish_layer(layer):
        last = layer == 1
        reduce_rows(2 * layer, o16, wdense, layer, dense_copy, not last)

        if last:
            flush(("spread", 0))

        @pl.when(owner)
        def _():
            add_rows(2 * layer, param_row(b_dense, layer))
            spread_rows(2 * layer, layer, 1)

        send_rows(2 * layer)
        bias = param_row(b_up, layer)
        for n in range(NCH):
            up_copy(layer, n).wait()
            take_rows(2 * layer, n)
            for c in range(4):
                at = slice(c * 1024, (c + 1) * 1024)
                piece = dot(u16[...], wup[n * CH:(n + 1) * CH, at])
                h_s[:, at] = piece + bias[:, at] if n == 0 else h_s[:, at] + piece
            if not last:
                up_copy(layer + 1, n).start()
        for c in range(4):
            pair = h_s[:, c * 1024:(c + 1) * 1024]
            gate = jnp.minimum(pair, GELU_LIMIT)
            line = jnp.clip(pltpu.roll(pair, 1023, 1), -GELU_LIMIT, GELU_LIMIT)
            act = gate * jax.nn.sigmoid(1.702 * gate) * (line + 1.0)
            act = jnp.where(lane % 2 == 0, act, 0.0).astype(BF16)
            for k in range(4):
                at = slice(c * 512 + k * 128, c * 512 + (k + 1) * 128)
                m16[:, at] = dot(act[:, k * 256:(k + 1) * 256], pick).astype(BF16)
        reduce_rows(2 * layer + 1, m16, wdown, layer, down_copy, not last)

    exchange(0, stats0)
    combine(0, stats0, q0[my_rows, :], kv0[my_rows, :])
    finish_layer(0)

    @pl.when(owner)
    def _():
        add_rows(1, param_row(b_down, 0))
        spread_rows(1, 1, 0)

    send_rows(1)
    some = acc.at[pl.ds(0, ROWS)]
    for n in range(NCH):
        qkv_copy(1, n).wait()
        take_rows(1, n)
        piece = dot(u16[...], wqkv[n * CH:(n + 1) * CH, :])
        some[...] = piece + param_row(b_qkv, 1) if n == 0 else some[...] + piece
    turn_columns(some, q1.at[s], kv1.at[s], cos_rows[my_rows, :], sin_rows[my_rows, :])
    for i, ref in enumerate((q1, kv1)):
        for d in (2, 1, 3):
            send(ref.at[s], ref.at[s], q_send.at[i, d - 1], q_recv.at[i, d - 1], "sp", lax.rem(s + d, 4))

    def gathered(i, ref):
        for d in range(1, 4):
            dst = ref.at[lax.rem(s - d + 4, 4)]
            arrived(dst, dst, q_send.at[i, d - 1], q_recv.at[i, d - 1], "sp", lax.rem(s + d, 4))

    gathered(0, q1)
    for i in range(4):
        for h in range(HEADS):
            q8[pl.ds(i * ROWS * 8 + h, ROWS, stride=8), :] = q1[i, :, h * HEAD:(h + 1) * HEAD]
    k_copy(1).wait()
    v_copy(1).wait()
    attend(False, pos_ref, q8, kbuf, vbuf, s8, acc8, ml8)
    pack_stats(stats1, acc8, ml8)
    exchange(1, stats1)
    combine(1, stats1, q1[s], kv1[s])
    finish_layer(1)

    twin = s + 1 - 2 * lax.rem(s, 2)
    across = lax.rem(s + 2, 4)
    diagonal = lax.rem(twin + 2, 4)

    def hop(kind, block, i, n, axis, peer):
        return block, block, fin_send.at[kind, i, n], fin_recv.at[kind, i, n], axis, peer

    for n in range(NCH):
        at = slice(n * CH, (n + 1) * CH)
        bias = param_row(b_down, 1)[:, at]

        @pl.when(owner)
        def _():
            fin[s, half, :, at] = round_bf16(x_own[:, at] + sum_rows(3, n) + bias)

        mine = fin.at[s, half, :, cols[n]]
        for d in range(1, 4):
            send(mine, mine, z_send.at[d - 1, n], fin_recv.at[0, half, n], "tp", lax.rem(t + d, 4), when=owner)
        for i in range(2):
            block = fin.at[s, i, :, cols[n]]

            @pl.when(t != i + 1)
            def _():
                arrived(*hop(0, block, i, n, "tp", lax.rem(t + 1, 4)))

            send(*hop(1, block, i, n, "sp", across))
            send(*hop(2, block, i, n, "sp", twin))
    for n in range(NCH):
        for i in range(2):
            block = fin.at[across, i, :, cols[n]]
            arrived(*hop(1, block, i, n, "sp", across))
            send(*hop(3, block, i, n, "sp", twin))
    gathered(1, kv1)
    for i in range(4):
        kv1_out[i * ROWS:(i + 1) * ROWS, :] = kv1[i]
    for n in range(NCH):
        for i in range(2):
            arrived(*hop(2, fin.at[twin, i, :, cols[n]], i, n, "sp", twin))
            arrived(*hop(3, fin.at[diagonal, i, :, cols[n]], i, n, "sp", twin))
    for i in range(4):
        hid[i * ROWS:(i + 1) * ROWS, :] = jnp.concatenate([fin[i, 0], fin[i, 1]], axis=0).astype(BF16)
    for key in list(unsent):
        flush(key)


def solution(mesh):
    cache_spec = P(None, "dp", "sp", "tp", None)
    in_specs = (P("dp", None), P("dp"), cache_spec, cache_spec, P(), P(), P(None, None, "tp"), P(None, "tp"),
                P(None, "tp", None), P(), P(None, None, "tp"), P(None, "tp"), P(None, "tp", None), P())
    out_specs = (P("dp", None), cache_spec, cache_spec)
    table = rope_table()
    vmem, smem, hbm = (pl.BlockSpec(memory_space=m) for m in (pltpu.VMEM, pltpu.SMEM, pl.ANY))
    dma = pltpu.SemaphoreType.DMA

    def device_step(hidden, positions, k_cache, v_cache, ln_gain, ln_bias, w_qkv, b_qkv, w_dense, b_dense,
                    w_up, b_up, w_down, b_down):
        flat = (2, SEQS, SLOTS * KV, HEAD)
        kc, vc = k_cache.reshape(flat), v_cache.reshape(flat)
        cache = jax.ShapeDtypeStruct(flat, BF16)
        row8 = [pltpu.VMEM((SEQS * 8, n * HEAD), F32) for n in (1, 2, 1, 1)]
        fresh = jax.ShapeDtypeStruct((SEQS, KVW), F32)
        hid, kv0, kv1 = pl.pallas_call(
            main_kernel,
            out_shape=(jax.ShapeDtypeStruct((SEQS, D), BF16), fresh, fresh),
            in_specs=[smem] + [vmem] * 8 + [hbm] * 6,
            out_specs=(vmem, vmem, vmem),
            scratch_shapes=[
                pltpu.VMEM((D, QKV), BF16), pltpu.VMEM((QW, D), BF16), pltpu.VMEM((D, UP), BF16),
                pltpu.VMEM((FF, D), BF16)] + [pltpu.VMEM(flat[1:], BF16)] * 2 + [
                pltpu.VMEM((2, 3, ROWS, STAT), F32),
                pltpu.VMEM((2, 2, OWN, D), F32),
                pltpu.VMEM((2, 3, OWN, D), F32),
                pltpu.VMEM((2, 2, OWN, D), F32),
                pltpu.VMEM((OWN, D), F32),
                pltpu.VMEM((ROWS, QW), BF16),
                pltpu.VMEM((ROWS, CH), BF16),
                pltpu.VMEM((ROWS, UP), F32),
                pltpu.VMEM((ROWS, FF), BF16),
                pltpu.VMEM((SEQS, D), BF16),
                pltpu.VMEM((SEQS, QKV), F32),
                pltpu.VMEM((SEQS, QW), F32),
                pltpu.VMEM((4, ROWS, QW), F32),
                pltpu.VMEM((4, ROWS, KVW), F32),
                pltpu.VMEM((SEQS, STAT), F32),
                pltpu.VMEM((SEQS, STAT), F32),
                pltpu.VMEM((4, 2, OWN, D), F32),
                pltpu.VMEM((SEQS, HEAD), F32), pltpu.VMEM((SEQS, HEAD), F32),
            ] + row8 + [
                dma((4, NCH)), dma((2,)), dma((2, 3)), dma((2, 3)), dma((4, 2, NCH)), dma((4, 3, NCH)),
                dma((3, 3, NCH)), dma((3, 2, NCH)), dma((2, 3)), dma((2, 3)), dma((4, 2, NCH)), dma((4, 2, NCH)),
                dma((3, NCH))],
            compiler_params=pltpu.CompilerParams(vmem_limit_bytes=VMEM_MAX, collective_id=0, has_side_effects=True),
            name="main",
        )(positions, hidden, ln_gain, ln_bias, b_qkv, b_dense, b_up, b_down, table,
          w_qkv, w_dense, w_up, w_down, kc, vc)

        hidden_out, ko, vo = pl.pallas_call(
            exit_kernel,
            out_shape=(jax.ShapeDtypeStruct((SEQS, D), BF16), cache, cache),
            in_specs=[smem, vmem, vmem, vmem, hbm, hbm],
            out_specs=(vmem, hbm, hbm),
            scratch_shapes=[pltpu.VMEM(flat, BF16)] * 2 + [dma((4, 2, NGRP))],
            compiler_params=pltpu.CompilerParams(vmem_limit_bytes=VMEM_MAX),
            name="exit",
        )(positions, kv0, kv1, hid, kc, vc)
        return hidden_out, ko.reshape(k_cache.shape), vo.reshape(v_cache.shape)

    return jax.shard_map(device_step, mesh=mesh, in_specs=in_specs, out_specs=out_specs, check_vma=False)
```

time: 102 us -> 115 us (1.13)
  Pallas kernels: 101 us -> 114 us
    pallas_call x1, Pallas kernels: 80.8 us -> 99.9 us  [device_step(): pl.pallas_call(main_kernel, out_shape=(jax.ShapeDtypeStruct((SEQS, D), BF...]
    pallas_call x1 -> x0, Pallas kernels: 11.8 us -> none  [device_step(): pl.pallas_call(entry_kernel, out_shape=(cache, cache, jax.ShapeDtypeStruc...]
    pallas_call x1, Pallas kernels: 8.44 us -> 14.2 us  [device_step(): pl.pallas_call(exit_kernel, out_shape=(jax.ShapeDtypeStruct((SEQS, D), BF...]
where the time goes in v2:
time: 115 us
  Pallas kernels  114 us (99%)
    pallas_call x1, Pallas kernels, device_step(): pl.pallas_call(main_kernel, out_shape=(jax.ShapeDtypeStruct((SEQS, D), BF...  99.9 us
    pallas_call x1, Pallas kernels, device_step(): pl.pallas_call(exit_kernel, out_shape=(jax.ShapeDtypeStruct((SEQS, D), BF...  14.2 us

profile of v2, /device:TPU:1, one launch (start us, length us, event | category | flops | bytes accessed | tf_op | source)
XLA Modules:
  0.0 114.8 jit_solution(15737751654551683639)
XLA Ops:
  0.6 99.9 %main.1 = (bf16[64,3072]{1,0:T(8,128)(2,1)}, f32[64,512]{1,0:T(8,128)}, f32[64,512]{1,0:T(8,128)}) custom-call(s32[64]{0:T(128)} %pos_ref.3, bf16[64,3072]{1,0:T(8,128)(2,1)} %hidden.1, bf16[2,2,3072]{2,1,0:T(2,128)(2,1)} %gain.1, bf16[2,2,3072]{2,1,0:T(2,128)(2,1)} %shift.1, bf16[2,1280]{1,0:T(2,128)(2,1)} %b_qkv.1, bf16[2,3072]{1,0:T(2,128)(2,1)} %b_dense.1, ...), custom_call_target="tpu_custom_call" | custom-call | tf_op jit(solution)/shard_map/main/pallas_call | solution.py:499
  100.5 14.2 %exit.1 = (bf16[64,3072]{1,0:T(8,128)(2,1)}, bf16[2,64,256,128]{3,2,1,0:T(8,128)(2,1)}, bf16[2,64,256,128]{3,2,1,0:T(8,128)(2,1)}) custom-call(s32[64]{0:T(128)} %pos_ref.3, f32[64,512]{1,0:T(8,128)} %get-tuple-element.9.kv0, f32[64,512]{1,0:T(8,128)} %get-tuple-element.10.kv1, bf16[64,3072]{1,0:T(8,128)(2,1)} %get-tuple-element.11.hid, ...), custom_call_target="tpu_custom_call" | custom-call | tf_op jit(solution)/shard_map/exit/pallas_call | solution.py:534

commit v3 on v2

v3 whole, which is shorter than its diff:
```python
import functools

import jax
import jax.numpy as jnp
import numpy as np
from jax import lax
from jax.experimental import pallas as pl
from jax.experimental.pallas import tpu as pltpu
from jax.sharding import PartitionSpec as P

MESH = pl.DeviceIdType.MESH
F32 = jnp.float32
BF16 = jnp.bfloat16
BLOCK_SIZE = 64
LOCAL_BLOCKS = 16
VERT_STRIDE = 8
ROPE_THETA = 1000000.0
GELU_LIMIT = 20.0
NORM_EPS = 0.00001
MASKED = -1e30

SEQS = 64
ROWS = 16
OWN = 4
SEQ_LEN = 512
SLOTS = 128
D = 3072
HEAD = 128
KV = 2
GROUP = 3
HEADS = KV * GROUP
QKV = 1280
QW = HEADS * HEAD
KVW = 2 * KV * HEAD
UP = 4096
FF = 2048
STAT = HEADS * HEAD + HEAD
NCH = 4
CH = D // NCH
GRP = 8
NGRP = SEQS // GRP
VMEM_MAX = 67043328


def rope_table():
    half = HEAD // 2
    inv = (ROPE_THETA ** (-np.arange(half).astype(np.float32) * np.float32(2.0 / HEAD))).astype(np.float32)
    angle = (np.arange(SEQ_LEN).astype(np.float32)[:, None] * inv[None, :]).astype(np.float64)
    cos, sin = np.cos(angle).astype(np.float32), np.sin(angle).astype(np.float32)
    return np.concatenate([cos, sin], 1)


def norm_rows(wide, gain, shift):
    mean = jnp.mean(wide, axis=-1, keepdims=True)
    centred = wide - mean
    var = jnp.mean(centred * centred, axis=-1, keepdims=True)
    return (centred * lax.rsqrt(var + NORM_EPS) * gain + shift).astype(BF16)


def param_row(ref, layer, which=None):
    rows = ref[...] if which is None else ref[layer]
    pick = layer if which is None else which
    return rows.astype(F32)[pick:pick + 1]


def round_bf16(x):
    return x.astype(BF16).astype(F32)


def dot(a, b):
    return jnp.dot(a, b, preferred_element_type=F32)


def turn_columns(acc, q_ref, kv_ref, cos, sin):
    for c in range(KV):
        for g in range(GROUP + 2):
            x = acc[:, (c * 5 + g) * HEAD:(c * 5 + g + 1) * HEAD]
            if g <= GROUP:
                x = x * cos + pltpu.roll(x, HEAD // 2, 1) * sin
            x = round_bf16(x)
            if g < GROUP:
                q_ref[:, (c * GROUP + g) * HEAD:(c * GROUP + g + 1) * HEAD] = x
            else:
                at = (c * 2 + g - GROUP) * HEAD
                kv_ref[:, at:at + HEAD] = x


def attend(sparse, pos_ref, q8, kbuf, vbuf, s8, acc8, ml8):
    t, s = lax.axis_index("tp"), lax.axis_index("sp")
    row = lax.broadcasted_iota(jnp.int32, (8, KV * SLOTS), 0)
    col = lax.broadcasted_iota(jnp.int32, (8, KV * SLOTS), 1)
    slot = s * SLOTS + col // KV
    same = (col % KV) == row // GROUP
    vertical = (slot // BLOCK_SIZE + (t * HEADS + row) + 1) % VERT_STRIDE == 0
    for b in range(SEQS):
        at = slice(b * 8, b * 8 + 8)
        p = pos_ref[b]
        scores = lax.dot_general(q8[at, :].astype(BF16), kbuf[b], (((1,), (1,)), ((), ())), preferred_element_type=F32)
        keep = (slot < p) & same
        if sparse:
            near = (p // BLOCK_SIZE - slot // BLOCK_SIZE) < LOCAL_BLOCKS
            keep = keep & (near | vertical)
        s8[at, :] = jnp.where(keep, scores * (1.0 / HEAD), -jnp.inf)
    for r in range(8):
        at = slice(r * SEQS, (r + 1) * SEQS)
        scores = s8[at, :]
        peak = jnp.maximum(jnp.max(scores, axis=-1, keepdims=True), MASKED)
        weights = jnp.exp(scores - peak)
        s8[at, :] = weights
        total = jnp.sum(weights, axis=-1, keepdims=True)
        low = lax.broadcasted_iota(jnp.int32, (SEQS, HEAD), 1) < HEADS
        ml8[at, :] = jnp.where(low, peak, total)
    for b in range(SEQS):
        at = slice(b * 8, b * 8 + 8)
        acc8[at, :] = dot(s8[at, :].astype(BF16), vbuf[b])


def pack_stats(stats, acc8, ml8):
    lane = lax.broadcasted_iota(jnp.int32, (SEQS, HEAD), 1)
    tail = jnp.zeros((SEQS, HEAD), F32)
    for h in range(HEADS):
        at = pl.ds(h, SEQS, stride=8)
        stats[:, h * HEAD:(h + 1) * HEAD] = acc8[at, :]
        tail = jnp.where((lane == h) | (lane == HEADS + h), ml8[at, :], tail)
    stats[:, HEADS * HEAD:] = tail


def put_new_rows(group, pos_ref, kv_ref, kbuf, vbuf):
    s = lax.axis_index("sp")
    row = lax.broadcasted_iota(jnp.int32, (16, HEAD), 0)
    fresh_rows = kv_ref[pl.ds(pl.multiple_of(group * GRP, GRP), GRP), :]
    for j in range(GRP):
        b = group * GRP + j
        local = pos_ref[b] - s * SLOTS
        inside = jnp.where((local >= 0) & (local < SLOTS), 1, 0)
        local = jnp.clip(local, 0, SLOTS - 1)
        at = pl.ds(pl.multiple_of((local // 8) * 16, 16), 16)
        target = jnp.where(inside == 1, local % 8, 99)
        hit = (row // KV) == target
        for i, buf in enumerate((kbuf, vbuf)):
            first, second = (fresh_rows[j:j + 1, (2 * c + i) * HEAD:(2 * c + i + 1) * HEAD] for c in range(KV))
            fresh = jnp.where(row % KV == 0, first, second)
            buf[b, at, :] = jnp.where(hit, fresh, buf[b, at, :].astype(F32)).astype(BF16)


def stream_cache(layer, src_pair, buf_pair, dst_pair, sems):
    def copies(g, out):
        at = pl.ds(g * GRP, GRP)
        if out:
            return [pltpu.make_async_copy(buf.at[at], dst.at[layer, at], sems.at[2 + i, g])
                    for i, (buf, dst) in enumerate(zip(buf_pair, dst_pair))]
        return [pltpu.make_async_copy(src.at[layer, at], buf.at[at], sems.at[i, g])
                for i, (src, buf) in enumerate(zip(src_pair, buf_pair))]

    return copies


def store_cache(copies, pos_ref, kv_ref, kbuf, vbuf):
    def one_group(g, carry):
        for copy in copies(g, 0):
            copy.wait()
        put_new_rows(g, pos_ref, kv_ref, kbuf, vbuf)
        for copy in copies(g, 1):
            copy.start()
        return carry

    lax.fori_loop(0, NGRP, one_group, 0)


def drain_cache(copies):
    def drain(g, carry):
        for copy in copies(g, 1):
            copy.wait()
        return carry

    lax.fori_loop(0, NGRP, drain, 0)


def fetch(sources, targets, sems):
    copies = [pltpu.make_async_copy(src, dst, sems.at[i]) for i, (src, dst) in enumerate(zip(sources, targets))]
    for copy in copies:
        copy.start()
    return copies


def entry_kernel(pos_hbm, hidden_hbm, gain_hbm, shift_hbm, b_hbm, table_hbm, w_hbm, kc_hbm, vc_hbm,
                 ko_hbm, vo_hbm, q0_hbm, kv0_hbm, stats0_hbm, cos_hbm, sin_hbm,
                 pos_ref, hidden, gain, shift, b_qkv, table, q0, kv0, stats0, cos_rows, sin_rows,
                 wbuf, kbuf, vbuf, u_s, acc, q8, s8, acc8, ml8, w_sem, sems, small):
    first = fetch((pos_hbm, hidden_hbm, gain_hbm, shift_hbm, b_hbm, table_hbm),
                  (pos_ref, hidden, gain, shift, b_qkv, table), small)
    copies = stream_cache(0, (kc_hbm, vc_hbm), (kbuf, vbuf), (ko_hbm, vo_hbm), sems)

    def w_copy(n):
        return pltpu.make_async_copy(w_hbm.at[0, pl.ds(n * CH, CH)], wbuf.at[pl.ds(n * CH, CH)], w_sem.at[n])

    for n in range(NCH):
        w_copy(n).start()

    q8[...] = jnp.zeros_like(q8)
    for copy in first:
        copy.wait()

    def pick_row(b, carry):
        p = pos_ref[b]
        cos_rows[pl.ds(b, 1), :] = table[pl.ds(p, 1), :]
        return carry

    lax.fori_loop(0, SEQS, pick_row, 0)
    both = cos_rows[...]
    other = pltpu.roll(both, HEAD // 2, 1)
    low = lax.broadcasted_iota(jnp.int32, (SEQS, HEAD), 1) < HEAD // 2
    cos_rows[...] = jnp.where(low, both, other)
    sin_rows[...] = jnp.where(low, -other, both)
    u_s[...] = norm_rows(hidden[...].astype(F32), param_row(gain, 0, 0), param_row(shift, 0, 0))
    for n in range(NCH):
        w_copy(n).wait()
        if n == 0:
            for g in range(NGRP):
                for copy in copies(g, 0):
                    copy.start()
        piece = dot(u_s[:, n * CH:(n + 1) * CH], wbuf[n * CH:(n + 1) * CH, :])
        acc[...] = piece + param_row(b_qkv, 0) if n == 0 else acc[...] + piece
    turn_columns(acc, q0, kv0, cos_rows[...], sin_rows[...])
    outs = fetch((q0, kv0, cos_rows, sin_rows), (q0_hbm, kv0_hbm, cos_hbm, sin_hbm), small)
    for h in range(HEADS):
        q8[pl.ds(h, SEQS, stride=8), :] = q0[:, h * HEAD:(h + 1) * HEAD]
    store_cache(copies, pos_ref, kv0, kbuf, vbuf)
    attend(True, pos_ref, q8, kbuf, vbuf, s8, acc8, ml8)
    pack_stats(stats0, acc8, ml8)
    stats_out = pltpu.make_async_copy(stats0, stats0_hbm, small.at[4])
    stats_out.start()
    drain_cache(copies)
    for copy in outs + [stats_out]:
        copy.wait()


def exit_kernel(pos_hbm, kv_hbm, hid_hbm, kc_hbm, vc_hbm, ka_hbm, va_hbm, hid_out, ko_hbm, vo_hbm,
                kbuf, vbuf, kv, hid, pos_ref, sems, small):
    copies = stream_cache(1, (kc_hbm, vc_hbm), (kbuf, vbuf), (ko_hbm, vo_hbm), sems)
    first = [pltpu.make_async_copy(src, dst, small.at[i])
             for i, (src, dst) in enumerate(((pos_hbm, pos_ref), (kv_hbm, kv), (hid_hbm, hid)))]
    hid_back = pltpu.make_async_copy(hid, hid_out, small.at[3])
    for copy in first:
        copy.start()
    for g in range(NGRP):
        for copy in copies(g, 0):
            copy.start()
    for copy in first:
        copy.wait()
    hid_back.start()
    store_cache(copies, pos_ref, kv, kbuf, vbuf)
    drain_cache(copies)
    hid_back.wait()


def main_kernel(pos_hbm, q0_hbm, kv0_hbm, stats0_hbm, cos_hbm, sin_hbm, hidden_hbm,
                gain_hbm, shift_hbm, bqkv_hbm, bdense_hbm, bup_hbm, bdown_hbm,
                wqkv_hbm, wdense_hbm, wup_hbm, wdown_hbm, kc_hbm, vc_hbm,
                hid, kv1_out,
                pos_ref, q0, kv0, stats0, cos_rows, sin_rows, hidden, gain, shift, b_qkv, b_dense, b_up, b_down, small,
                wqkv, wdense, wup, wdown, kbuf, vbuf,
                mix, part, summed, spread, x_own, o16, u16, h_s, m16, acc, q1, kv1, stats1, fin, q8, s8, acc8, ml8,
                w_sem, kv_sem, mix_send, mix_recv, part_send, part_recv, spread_send, spread_recv,
                q_send, q_recv, fin_send, fin_recv, z_send):
    t, s = lax.axis_index("tp"), lax.axis_index("sp")
    far = (2, 1, 3)
    unsent = {}

    def remote(src, dst, send_sem, recv_sem, axis, peer):
        return pltpu.make_async_remote_copy(src_ref=src, dst_ref=dst, send_sem=send_sem, recv_sem=recv_sem,
                                            device_id={axis: peer}, device_id_type=MESH)

    def send(*args, key=None):
        copy = remote(*args)
        copy.start()
        unsent.setdefault(key, []).append(copy)

    def flush(key):
        for copy in unsent.pop(key):
            copy.wait_send()

    def arrived(*args):
        remote(*args).wait_recv()

    barrier = pltpu.get_barrier_semaphore()
    for axis, me in (("tp", t), ("sp", s)):
        for d in range(1, 4):
            pl.semaphore_signal(barrier, inc=1, device_id={axis: lax.rem(me + d, 4)}, device_id_type=MESH)

    my_rows = pl.ds(pl.multiple_of(s * ROWS, ROWS), ROWS)
    first = fetch((stats0_hbm, pos_hbm, q0_hbm.at[my_rows], kv0_hbm.at[my_rows], cos_hbm.at[my_rows],
                   sin_hbm.at[my_rows], hidden_hbm.at[my_rows], gain_hbm, shift_hbm, bqkv_hbm, bdense_hbm, bup_hbm,
                   bdown_hbm),
                  (stats0, pos_ref, q0, kv0, cos_rows, sin_rows, hidden, gain, shift, b_qkv, b_dense, b_up, b_down),
                  small)
    cols = [pl.ds(n * CH, CH) for n in range(NCH)]

    def dense_copy(layer, n):
        return pltpu.make_async_copy(wdense_hbm.at[layer, :, cols[n]], wdense.at[:, cols[n]], w_sem.at[0, n])

    def up_copy(layer, n):
        return pltpu.make_async_copy(wup_hbm.at[layer, cols[n]], wup.at[cols[n]], w_sem.at[1, n])

    def down_copy(layer, n):
        return pltpu.make_async_copy(wdown_hbm.at[layer, :, cols[n]], wdown.at[:, cols[n]], w_sem.at[2, n])

    def qkv_copy(layer, n):
        return pltpu.make_async_copy(wqkv_hbm.at[layer, cols[n]], wqkv.at[cols[n]], w_sem.at[3, n])

    def k_copy(layer):
        return pltpu.make_async_copy(kc_hbm.at[layer], kbuf, kv_sem.at[0])

    def v_copy(layer):
        return pltpu.make_async_copy(vc_hbm.at[layer], vbuf, kv_sem.at[1])

    q8[...] = jnp.zeros_like(q8)
    for copy in first:
        copy.wait()
    for n in range(NCH):
        dense_copy(0, n).start()
    for n in range(NCH):
        up_copy(0, n).start()
    wide = hidden[...].astype(F32)
    for j in range(4):
        fin[0, j] = wide[OWN * j:OWN * (j + 1)]
    x_own[...] = fin[0, t]
    pl.semaphore_wait(barrier, 6)

    def exchange(layer, stats):
        for d in far:
            peer = lax.rem(s + d, 4)
            rows = pl.ds(pl.multiple_of(peer * ROWS, ROWS), ROWS)
            send(stats.at[rows], mix.at[layer, d - 1], mix_send.at[layer, d - 1], mix_recv.at[layer, d - 1], "sp", peer)

    def combine(layer, stats, q_rows, kv_rows):
        for d in range(1, 4):
            arrived(mix.at[layer, d - 1], mix.at[layer, d - 1], mix_send.at[layer, d - 1], mix_recv.at[layer, d - 1],
                    "sp", lax.rem(s + d, 4))
        shards = [stats[my_rows, :]] + [mix[layer, d] for d in range(3)]
        for h in range(HEADS):
            c = h // GROUP
            q = q_rows[:, h * HEAD:(h + 1) * HEAD]
            k = kv_rows[:, 2 * c * HEAD:(2 * c + 1) * HEAD]
            v = kv_rows[:, (2 * c + 1) * HEAD:(2 * c + 2) * HEAD]
            fresh = jnp.sum(q * k, axis=-1, keepdims=True) * (1.0 / HEAD)
            peaks = [x[:, QW + h:QW + h + 1] for x in shards]
            top = fresh
            for peak in peaks:
                top = jnp.maximum(top, peak)
            scale = jnp.exp(fresh - top)
            num, den = v * scale, scale
            for x, peak in zip(shards, peaks):
                scale = jnp.exp(peak - top)
                num = num + x[:, h * HEAD:(h + 1) * HEAD] * scale
                den = den + x[:, QW + HEADS + h:QW + HEADS + h + 1] * scale
            o16[:, h * HEAD:(h + 1) * HEAD] = (num / den).astype(BF16)

    def reduce_rows(phase, lhs, weights, layer, copy_of):
        turn = phase % 2
        if phase >= 2:
            flush(("part", phase - 2))
        for n in range(NCH):
            copy_of(layer, n).wait()
            piece = dot(lhs[...], weights[:, n * CH:(n + 1) * CH])
            for j in range(4):
                part[turn, j, :, n * CH:(n + 1) * CH] = piece[OWN * j:OWN * (j + 1)]
            for d in far:
                peer = lax.rem(t + d, 4)
                send(part.at[turn, peer, :, cols[n]], summed.at[turn, d - 1, :, cols[n]],
                     part_send.at[phase, d - 1, n], part_recv.at[phase, d - 1, n], "tp", peer, key=("part", phase))

    def sum_rows(phase, n):
        turn = phase % 2
        for d in range(1, 4):
            dst = summed.at[turn, d - 1, :, cols[n]]
            arrived(dst, dst, part_send.at[phase, d - 1, n], part_recv.at[phase, d - 1, n], "tp", lax.rem(t + d, 4))
        at = slice(n * CH, (n + 1) * CH)
        return part[turn, t, :, at] + summed[turn, 0, :, at] + summed[turn, 1, :, at] + summed[turn, 2, :, at]

    def add_rows(phase, bias):
        for n in range(NCH):
            at = slice(n * CH, (n + 1) * CH)
            x_own[:, at] = round_bf16(x_own[:, at] + sum_rows(phase, n) + bias[:, at])

    def spread_rows(phase, layer, which):
        rows = norm_rows(x_own[...], param_row(gain, layer, which), param_row(shift, layer, which))
        spread[phase % 2, t] = rows.astype(F32)
        for n in range(NCH):
            block = spread.at[phase % 2, t, :, cols[n]]
            for d in far:
                send(block, block, spread_send.at[phase, d - 1, n], spread_recv.at[phase, d - 1, n], "tp",
                     lax.rem(t + d, 4), key=("spread", phase))

    def take_rows(phase, n):
        for d in range(1, 4):
            dst = spread.at[phase % 2, lax.rem(t - d + 4, 4), :, cols[n]]
            arrived(dst, dst, spread_send.at[phase, d - 1, n], spread_recv.at[phase, d - 1, n], "tp", lax.rem(t + d, 4))
        at = slice(n * CH, (n + 1) * CH)
        u16[...] = jnp.concatenate([spread[phase % 2, j, :, at] for j in range(4)], axis=0).astype(BF16)

    lane = lax.broadcasted_iota(jnp.int32, (ROWS, 1024), 1)
    pick = (lax.broadcasted_iota(jnp.int32, (256, 128), 0) == 2 * lax.broadcasted_iota(jnp.int32, (256, 128), 1))
    pick = jnp.where(pick, 1.0, 0.0).astype(BF16)

    def finish_layer(layer):
        last = layer == 1
        reduce_rows(2 * layer, o16, wdense, layer, dense_copy)

        if last:
            flush(("spread", 0))

        add_rows(2 * layer, param_row(b_dense, layer))
        spread_rows(2 * layer, layer, 1)
        bias = param_row(b_up, layer)
        for n in range(NCH):
            up_copy(layer, n).wait()
            take_rows(2 * layer, n)
            for c in range(4):
                at = slice(c * 1024, (c + 1) * 1024)
                piece = dot(u16[...], wup[n * CH:(n + 1) * CH, at])
                h_s[:, at] = piece + bias[:, at] if n == 0 else h_s[:, at] + piece
        if not last:
            for n in range(NCH):
                qkv_copy(1, n).start()
        for c in range(4):
            pair = h_s[:, c * 1024:(c + 1) * 1024]
            gate = jnp.minimum(pair, GELU_LIMIT)
            line = jnp.clip(pltpu.roll(pair, 1023, 1), -GELU_LIMIT, GELU_LIMIT)
            act = gate * jax.nn.sigmoid(1.702 * gate) * (line + 1.0)
            act = jnp.where(lane % 2 == 0, act, 0.0).astype(BF16)
            for k in range(4):
                at = slice(c * 512 + k * 128, c * 512 + (k + 1) * 128)
                m16[:, at] = dot(act[:, k * 256:(k + 1) * 256], pick).astype(BF16)
        reduce_rows(2 * layer + 1, m16, wdown, layer, down_copy)
        if not last:
            k_copy(1).start()
            v_copy(1).start()

    exchange(0, stats0)
    for n in range(NCH):
        down_copy(0, n).start()
    combine(0, stats0, q0[...], kv0[...])
    finish_layer(0)

    add_rows(1, param_row(b_down, 0))
    spread_rows(1, 1, 0)
    for n in range(NCH):
        qkv_copy(1, n).wait()
        take_rows(1, n)
        piece = dot(u16[...], wqkv[n * CH:(n + 1) * CH, :])
        acc[...] = piece + param_row(b_qkv, 1) if n == 0 else acc[...] + piece
    for n in range(NCH):
        dense_copy(1, n).start()
    for n in range(NCH):
        up_copy(1, n).start()
    turn_columns(acc, q1.at[s], kv1.at[s], cos_rows[...], sin_rows[...])
    for i, ref in enumerate((q1, kv1)):
        for d in far:
            send(ref.at[s], ref.at[s], q_send.at[i, d - 1], q_recv.at[i, d - 1], "sp", lax.rem(s + d, 4))

    def gathered(i, ref):
        for d in range(1, 4):
            dst = ref.at[lax.rem(s - d + 4, 4)]
            arrived(dst, dst, q_send.at[i, d - 1], q_recv.at[i, d - 1], "sp", lax.rem(s + d, 4))

    gathered(0, q1)
    for i in range(4):
        for h in range(HEADS):
            q8[pl.ds(i * ROWS * 8 + h, ROWS, stride=8), :] = q1[i, :, h * HEAD:(h + 1) * HEAD]
    k_copy(1).wait()
    v_copy(1).wait()
    attend(False, pos_ref, q8, kbuf, vbuf, s8, acc8, ml8)
    pack_stats(stats1, acc8, ml8)
    for n in range(NCH):
        down_copy(1, n).start()
    exchange(1, stats1)
    combine(1, stats1, q1[s], kv1[s])
    finish_layer(1)

    twin = s + 1 - 2 * lax.rem(s, 2)
    across = lax.rem(s + 2, 4)
    diagonal = lax.rem(twin + 2, 4)

    def hop(kind, block, i, n, axis, peer):
        return block, block, fin_send.at[kind, i, n], fin_recv.at[kind, i, n], axis, peer

    bias = param_row(b_down, 1)
    for n in range(NCH):
        at = slice(n * CH, (n + 1) * CH)
        fin[s, t, :, at] = round_bf16(x_own[:, at] + sum_rows(3, n) + bias[:, at])
        block = fin.at[s, t, :, cols[n]]
        for d in far:
            send(block, block, z_send.at[d - 1, n], fin_recv.at[0, d, n], "tp", lax.rem(t + d, 4))
        send(*hop(1, block, 0, n, "sp", across))
        send(*hop(2, block, 0, n, "sp", twin))
    for n in range(NCH):
        for d in (1, 3, 2):
            block = fin.at[s, lax.rem(t - d + 4, 4), :, cols[n]]
            arrived(*hop(0, block, d, n, "tp", lax.rem(t + d, 4)))
            send(*hop(1, block, d, n, "sp", across))
            send(*hop(2, block, d, n, "sp", twin))
    for n in range(NCH):
        for d in range(4):
            block = fin.at[across, lax.rem(t - d + 4, 4), :, cols[n]]
            arrived(*hop(1, block, d, n, "sp", across))
            send(*hop(3, block, d, n, "sp", twin))
    gathered(1, kv1)
    for i in range(4):
        kv1_out[i * ROWS:(i + 1) * ROWS, :] = kv1[i]
    for n in range(NCH):
        for d in range(4):
            arrived(*hop(2, fin.at[twin, lax.rem(t - d + 4, 4), :, cols[n]], d, n, "sp", twin))
            arrived(*hop(3, fin.at[diagonal, lax.rem(t - d + 4, 4), :, cols[n]], d, n, "sp", twin))
    for i in range(4):
        hid[i * ROWS:(i + 1) * ROWS, :] = jnp.concatenate([fin[i, j] for j in range(4)], axis=0).astype(BF16)
    for key in list(unsent):
        flush(key)


def solution(mesh):
    cache_spec = P(None, "dp", "sp", "tp", None)
    in_specs = (P("dp", None), P("dp"), cache_spec, cache_spec, P(), P(), P(None, None, "tp"), P(None, "tp"),
                P(None, "tp", None), P(), P(None, None, "tp"), P(None, "tp"), P(None, "tp", None), P())
    out_specs = (P("dp", None), cache_spec, cache_spec)
    table = rope_table()
    vmem, hbm = (pl.BlockSpec(memory_space=m) for m in (pltpu.VMEM, pl.ANY))
    dma = pltpu.SemaphoreType.DMA

    def device_step(hidden, positions, k_cache, v_cache, ln_gain, ln_bias, w_qkv, b_qkv, w_dense, b_dense,
                    w_up, b_up, w_down, b_down):
        flat = (2, SEQS, SLOTS * KV, HEAD)
        kc, vc = k_cache.reshape(flat), v_cache.reshape(flat)
        cache = jax.ShapeDtypeStruct(flat, BF16)
        row8 = [pltpu.VMEM((SEQS * 8, n * HEAD), F32) for n in (1, 2, 1, 1)]
        buffers = [pltpu.VMEM(flat[1:], BF16)] * 2
        rows = [jax.ShapeDtypeStruct((SEQS, n), F32) for n in (QW, KVW, STAT, HEAD, HEAD)]
        big = pltpu.CompilerParams(vmem_limit_bytes=VMEM_MAX)
        ko, vo, q0, kv0, stats0, cos_rows, sin_rows = pl.pallas_call(
            entry_kernel,
            out_shape=(cache, cache, *rows),
            in_specs=[hbm] * 9,
            out_specs=(hbm,) * 7,
            scratch_shapes=[pltpu.SMEM((SEQS,), jnp.int32), pltpu.VMEM((SEQS, D), BF16), pltpu.VMEM((2, 2, D), BF16),
                            pltpu.VMEM((2, 2, D), BF16), pltpu.VMEM((2, QKV), BF16), pltpu.VMEM((SEQ_LEN, HEAD), F32)]
            + [pltpu.VMEM(x.shape, F32) for x in rows] + [pltpu.VMEM((D, QKV), BF16)] + buffers
            + [pltpu.VMEM((SEQS, D), BF16), pltpu.VMEM((SEQS, QKV), F32)] + row8 + [dma((NCH,)), dma((4, NGRP)), dma((6,))],
            compiler_params=big,
            name="entry",
        )(positions, hidden, ln_gain, ln_bias, b_qkv, table, w_qkv, kc, vc)

        hid, kv1 = pl.pallas_call(
            main_kernel,
            out_shape=(jax.ShapeDtypeStruct((SEQS, D), BF16), rows[1]),
            in_specs=[hbm] * 19,
            out_specs=(vmem, vmem),
            scratch_shapes=[
                pltpu.SMEM((SEQS,), jnp.int32), pltpu.VMEM((ROWS, QW), F32), pltpu.VMEM((ROWS, KVW), F32),
                pltpu.VMEM((SEQS, STAT), F32), pltpu.VMEM((ROWS, HEAD), F32), pltpu.VMEM((ROWS, HEAD), F32),
                pltpu.VMEM((ROWS, D), BF16), pltpu.VMEM((2, 2, D), BF16), pltpu.VMEM((2, 2, D), BF16),
                pltpu.VMEM((2, QKV), BF16), pltpu.VMEM((2, D), BF16), pltpu.VMEM((2, UP), BF16),
                pltpu.VMEM((2, D), BF16), dma((13,)),
                pltpu.VMEM((D, QKV), BF16), pltpu.VMEM((QW, D), BF16), pltpu.VMEM((D, UP), BF16),
                pltpu.VMEM((FF, D), BF16)] + buffers + [
                pltpu.VMEM((2, 3, ROWS, STAT), F32),
                pltpu.VMEM((2, 4, OWN, D), F32),
                pltpu.VMEM((2, 3, OWN, D), F32),
                pltpu.VMEM((2, 4, OWN, D), F32),
                pltpu.VMEM((OWN, D), F32),
                pltpu.VMEM((ROWS, QW), BF16),
                pltpu.VMEM((ROWS, CH), BF16),
                pltpu.VMEM((ROWS, UP), F32),
                pltpu.VMEM((ROWS, FF), BF16),
                pltpu.VMEM((ROWS, QKV), F32),
                pltpu.VMEM((4, ROWS, QW), F32),
                pltpu.VMEM((4, ROWS, KVW), F32),
                pltpu.VMEM((SEQS, STAT), F32),
                pltpu.VMEM((4, 4, OWN, D), F32),
            ] + row8 + [
                dma((4, NCH)), dma((2,)), dma((2, 3)), dma((2, 3)), dma((4, 3, NCH)), dma((4, 3, NCH)),
                dma((3, 3, NCH)), dma((3, 3, NCH)), dma((2, 3)), dma((2, 3)), dma((4, 4, NCH)), dma((4, 4, NCH)),
                dma((3, NCH))],
            compiler_params=pltpu.CompilerParams(vmem_limit_bytes=VMEM_MAX, collective_id=0, has_side_effects=True),
            name="main",
        )(positions, q0, kv0, stats0, cos_rows, sin_rows, hidden, ln_gain, ln_bias, b_qkv, b_dense, b_up, b_down,
          w_qkv, w_dense, w_up, w_down, kc, vc)

        hidden_out, ko, vo = pl.pallas_call(
            exit_kernel,
            out_shape=(jax.ShapeDtypeStruct((SEQS, D), BF16), cache, cache),
            in_specs=[hbm] * 7,
            out_specs=(hbm, hbm, hbm),
            scratch_shapes=buffers + [pltpu.VMEM((SEQS, KVW), F32), pltpu.VMEM((SEQS, D), BF16),
                                      pltpu.SMEM((SEQS,), jnp.int32), dma((4, NGRP)), dma((4,))],
            input_output_aliases={5: 1, 6: 2},
            compiler_params=big,
            name="exit",
        )(positions, kv1, hid, kc, vc, ko, vo)
        return hidden_out, ko.reshape(k_cache.shape), vo.reshape(v_cache.shape)

    return jax.shard_map(device_step, mesh=mesh, in_specs=in_specs, out_specs=out_specs, check_vma=False)
```

time: 115 us -> 100 us (0.87)
  Pallas kernels: 114 us -> 99 us
    pallas_call x1, Pallas kernels: 99.9 us -> 79.9 us  [device_step(): pl.pallas_call(main_kernel, out_shape=(jax.ShapeDtypeStruct((SEQS, D), BF...]
    pallas_call x0 -> x1, Pallas kernels: none -> 12.1 us  [device_step(): pl.pallas_call(entry_kernel, out_shape=(cache, cache, *rows), in_specs=[h...]
    pallas_call x1, Pallas kernels: 14.2 us -> 7.09 us  [device_step(): pl.pallas_call(exit_kernel, out_shape=(jax.ShapeDtypeStruct((SEQS, D), BF...]
where the time goes in v3:
time: 100 us; the launch traced here: 99.8 us
  Pallas kernels  99 us (99%)
    pallas_call x1, Pallas kernels, device_step(): pl.pallas_call(main_kernel, out_shape=(jax.ShapeDtypeStruct((SEQS, D), BF...  79.9 us
    pallas_call x1, Pallas kernels, device_step(): pl.pallas_call(entry_kernel, out_shape=(cache, cache, *rows), in_specs=[h...  12.1 us
    pallas_call x1, Pallas kernels, device_step(): pl.pallas_call(exit_kernel, out_shape=(jax.ShapeDtypeStruct((SEQS, D), BF...  7.09 us

profile of v3, /device:TPU:1, one launch (start us, length us, event | category | flops | bytes accessed | tf_op | source)
XLA Modules:
  0.0 99.8 jit_solution(9932179132569236729)
XLA Ops:
  0.6 12.1 %entry.1 = (bf16[2,64,256,128]{3,2,1,0:T(8,128)(2,1)}, bf16[2,64,256,128]{3,2,1,0:T(8,128)(2,1)}, f32[64,768]{1,0:T(8,128)}, f32[64,512]{1,0:T(8,128)}, f32[64,8...) custom-call(s32[64]{0:T(128)} %pos_hbm.5, bf16[64,3072]{1,0:T(8,128)(2,1)} %hidden_hbm.3, ...), custom_call_target="tpu_custom_call" | custom-call | tf_op jit(solution)/shard_map/entry/pallas_call | solution.py:539
  12.7 79.9 %main.1 = (bf16[64,3072]{1,0:T(8,128)(2,1)}, f32[64,512]{1,0:T(8,128)}) custom-call(s32[64]{0:T(128)} %pos_hbm.5, f32[64,768]{1,0:T(8,128)} %get-tuple-element.15.q0_hbm, f32[64,512]{1,0:T(8,128)} %get-tuple-element.16.kv0_hbm, f32[64,896]{1,0:T(8,128)} %get-tuple-element.17.stats0_hbm, f32[64,128]{1,0:T(8,128)} %get-tuple-element.18.cos_hbm, ...), custom_call_target="tpu_custom_call" | custom-call | tf_op jit(solution)/shard_map/main/pallas_call | solution.py:552
  92.6 7.1 %exit.1 = (bf16[64,3072]{1,0:T(8,128)(2,1)}, bf16[2,64,256,128]{3,2,1,0:T(8,128)(2,1)}, bf16[2,64,256,128]{3,2,1,0:T(8,128)(2,1)}) custom-call(s32[64]{0:T(128)} %pos_hbm.5, f32[64,512]{1,0:T(8,128)} %get-tuple-element.20.kv_hbm, bf16[64,3072]{1,0:T(8,128)(2,1)} %get-tuple-element.21.hid_hbm, ...), custom_call_target="tpu_custom_call", output_to_operand_aliasing={{1}: (5, {}), {2}: (6, {})} | custom-call | tf_op jit(solution)/shard_map/exit/pallas_call | solution.py:588

commit v4 on v3

--- a/solution.py
+++ b/solution.py
@@ -85,24 +85,26 @@
                 kv_ref[:, at:at + HEAD] = x
 
 
-def attend(sparse, pos_ref, q8, kbuf, vbuf, s8, acc8, ml8):
+def attend(sparse, base, count, start, pos_ref, q8, kbuf, vbuf, s8, acc8, ml8):
     t, s = lax.axis_index("tp"), lax.axis_index("sp")
     row = lax.broadcasted_iota(jnp.int32, (8, KV * SLOTS), 0)
     col = lax.broadcasted_iota(jnp.int32, (8, KV * SLOTS), 1)
     slot = s * SLOTS + col // KV
     same = (col % KV) == row // GROUP
     vertical = (slot // BLOCK_SIZE + (t * HEADS + row) + 1) % VERT_STRIDE == 0
-    for b in range(SEQS):
-        at = slice(b * 8, b * 8 + 8)
+    for j in range(count):
+        at = slice((start + j) * 8, (start + j) * 8 + 8)
+        b = base + j
         p = pos_ref[b]
-        scores = lax.dot_general(q8[at, :].astype(BF16), kbuf[b], (((1,), (1,)), ((), ())), preferred_element_type=F32)
+        queries = q8[pl.ds(pl.multiple_of(b * 8, 8), 8), :].astype(BF16)
+        scores = lax.dot_general(queries, kbuf[b], (((1,), (1,)), ((), ())), preferred_element_type=F32)
         keep = (slot < p) & same
         if sparse:
             near = (p // BLOCK_SIZE - slot // BLOCK_SIZE) < LOCAL_BLOCKS
             keep = keep & (near | vertical)
         s8[at, :] = jnp.where(keep, scores * (1.0 / HEAD), -jnp.inf)
-    for r in range(8):
-        at = slice(r * SEQS, (r + 1) * SEQS)
+    for r in range(count // 8):
+        at = slice(start * 8 + r * SEQS, start * 8 + (r + 1) * SEQS)
         scores = s8[at, :]
         peak = jnp.maximum(jnp.max(scores, axis=-1, keepdims=True), MASKED)
         weights = jnp.exp(scores - peak)
@@ -110,19 +112,20 @@
         total = jnp.sum(weights, axis=-1, keepdims=True)
         low = lax.broadcasted_iota(jnp.int32, (SEQS, HEAD), 1) < HEADS
         ml8[at, :] = jnp.where(low, peak, total)
-    for b in range(SEQS):
-        at = slice(b * 8, b * 8 + 8)
-        acc8[at, :] = dot(s8[at, :].astype(BF16), vbuf[b])
-
-
-def pack_stats(stats, acc8, ml8):
-    lane = lax.broadcasted_iota(jnp.int32, (SEQS, HEAD), 1)
-    tail = jnp.zeros((SEQS, HEAD), F32)
+    for j in range(count):
+        at = slice((start + j) * 8, (start + j) * 8 + 8)
+        acc8[at, :] = dot(s8[at, :].astype(BF16), vbuf[base + j])
+
+
+def pack_stats(stats, base, count, start, acc8, ml8):
+    rows = slice(base, base + count) if isinstance(base, int) else pl.ds(pl.multiple_of(base, count), count)
+    lane = lax.broadcasted_iota(jnp.int32, (count, HEAD), 1)
+    tail = jnp.zeros((count, HEAD), F32)
     for h in range(HEADS):
-        at = pl.ds(h, SEQS, stride=8)
-        stats[:, h * HEAD:(h + 1) * HEAD] = acc8[at, :]
+        at = pl.ds(start * 8 + h, count, stride=8)
+        stats[rows, h * HEAD:(h + 1) * HEAD] = acc8[at, :]
         tail = jnp.where((lane == h) | (lane == HEADS + h), ml8[at, :], tail)
-    stats[:, HEADS * HEAD:] = tail
+    stats[rows, HEADS * HEAD:] = tail
 
 
 def put_new_rows(group, pos_ref, kv_ref, kbuf, vbuf):
@@ -226,8 +229,8 @@
     for h in range(HEADS):
         q8[pl.ds(h, SEQS, stride=8), :] = q0[:, h * HEAD:(h + 1) * HEAD]
     store_cache(copies, pos_ref, kv0, kbuf, vbuf)
-    attend(True, pos_ref, q8, kbuf, vbuf, s8, acc8, ml8)
-    pack_stats(stats0, acc8, ml8)
+    attend(True, 0, SEQS, 0, pos_ref, q8, kbuf, vbuf, s8, acc8, ml8)
+    pack_stats(stats0, 0, SEQS, 0, acc8, ml8)
     stats_out = pltpu.make_async_copy(stats0, stats0_hbm, small.at[4])
     stats_out.start()
     drain_cache(copies)
@@ -327,16 +330,20 @@
     x_own[...] = fin[0, t]
     pl.semaphore_wait(barrier, 6)
 
-    def exchange(layer, stats):
-        for d in far:
-            peer = lax.rem(s + d, 4)
+    twin = s + 1 - 2 * (s % 2)
+    across = (s + 2) % 4
+    partners = (twin, across, (twin + 2) % 4)
+
+    def exchange(layer, stats, kinds):
+        for kind in kinds:
+            peer = partners[kind]
             rows = pl.ds(pl.multiple_of(peer * ROWS, ROWS), ROWS)
-            send(stats.at[rows], mix.at[layer, d - 1], mix_send.at[layer, d - 1], mix_recv.at[layer, d - 1], "sp", peer)
+            send(stats.at[rows], mix.at[layer, kind], mix_send.at[layer, kind], mix_recv.at[layer, kind], "sp", peer)
 
     def combine(layer, stats, q_rows, kv_rows):
-        for d in range(1, 4):
-            arrived(mix.at[layer, d - 1], mix.at[layer, d - 1], mix_send.at[layer, d - 1], mix_recv.at[layer, d - 1],
-                    "sp", lax.rem(s + d, 4))
+        for kind in range(3):
+            dst = mix.at[layer, kind]
+            arrived(dst, dst, mix_send.at[layer, kind], mix_recv.at[layer, kind], "sp", partners[kind])
         shards = [stats[my_rows, :]] + [mix[layer, d] for d in range(3)]
         for h in range(HEADS):
             c = h // GROUP
@@ -437,7 +444,7 @@
             k_copy(1).start()
             v_copy(1).start()
 
-    exchange(0, stats0)
+    exchange(0, stats0, (2, 1, 0))
     for n in range(NCH):
         down_copy(0, n).start()
     combine(0, stats0, q0[...], kv0[...])
@@ -470,16 +477,16 @@
             q8[pl.ds(i * ROWS * 8 + h, ROWS, stride=8), :] = q1[i, :, h * HEAD:(h + 1) * HEAD]
     k_copy(1).wait()
     v_copy(1).wait()
-    attend(False, pos_ref, q8, kbuf, vbuf, s8, acc8, ml8)
-    pack_stats(stats1, acc8, ml8)
+    half = SEQS // 2
+    for i, (base, kinds) in enumerate((((1 - s // 2) * half, (2, 1)), ((s // 2) * half, (0,)))):
+        attend(False, base, half, i * half, pos_ref, q8, kbuf, vbuf, s8, acc8, ml8)
+        pack_stats(stats1, base, half, i * half, acc8, ml8)
+        exchange(1, stats1, kinds)
     for n in range(NCH):
         down_copy(1, n).start()
-    exchange(1, stats1)
     combine(1, stats1, q1[s], kv1[s])
     finish_layer(1)
 
-    twin = s + 1 - 2 * lax.rem(s, 2)
-    across = lax.rem(s + 2, 4)
     diagonal = lax.rem(twin + 2, 4)
 
     def hop(kind, block, i, n, axis, peer):

time: 100 us -> 98.6 us (0.986)
  Pallas kernels: 99 us -> 97.7 us
    pallas_call x1, Pallas kernels: 79.9 us -> 78.5 us  [device_step(): pl.pallas_call(main_kernel, out_shape=(jax.ShapeDtypeStruct((SEQS, D), BF...]
where the time goes in v4:
time: 98.6 us; the launch traced here: 98.5 us
  Pallas kernels  97.7 us (99%)
    pallas_call x1, Pallas kernels, device_step(): pl.pallas_call(main_kernel, out_shape=(jax.ShapeDtypeStruct((SEQS, D), BF...  78.5 us
    pallas_call x1, Pallas kernels, device_step(): pl.pallas_call(entry_kernel, out_shape=(cache, cache, *rows), in_specs=[h...  12.1 us
    pallas_call x1, Pallas kernels, device_step(): pl.pallas_call(exit_kernel, out_shape=(jax.ShapeDtypeStruct((SEQS, D), BF...  7.09 us

profile of v4, /device:TPU:1, one launch (start us, length us, event | category | flops | bytes accessed | tf_op | source)
XLA Modules:
  0.0 98.5 jit_solution(11101291200494398581)
XLA Ops:
  0.6 12.1 %entry.1 = (bf16[2,64,256,128]{3,2,1,0:T(8,128)(2,1)}, bf16[2,64,256,128]{3,2,1,0:T(8,128)(2,1)}, f32[64,768]{1,0:T(8,128)}, f32[64,512]{1,0:T(8,128)}, f32[64,8...) custom-call(s32[64]{0:T(128)} %pos_hbm.5, bf16[64,3072]{1,0:T(8,128)(2,1)} %hidden_hbm.3, ...), custom_call_target="tpu_custom_call" | custom-call | tf_op jit(solution)/shard_map/entry/pallas_call | solution.py:546
  12.7 78.5 %main.1 = (bf16[64,3072]{1,0:T(8,128)(2,1)}, f32[64,512]{1,0:T(8,128)}) custom-call(s32[64]{0:T(128)} %pos_hbm.5, f32[64,768]{1,0:T(8,128)} %get-tuple-element.15.q0_hbm, f32[64,512]{1,0:T(8,128)} %get-tuple-element.16.kv0_hbm, f32[64,896]{1,0:T(8,128)} %get-tuple-element.17.stats0_hbm, f32[64,128]{1,0:T(8,128)} %get-tuple-element.18.cos_hbm, ...), custom_call_target="tpu_custom_call" | custom-call | tf_op jit(solution)/shard_map/main/pallas_call | solution.py:559
  91.2 7.1 %exit.1 = (bf16[64,3072]{1,0:T(8,128)(2,1)}, bf16[2,64,256,128]{3,2,1,0:T(8,128)(2,1)}, bf16[2,64,256,128]{3,2,1,0:T(8,128)(2,1)}) custom-call(s32[64]{0:T(128)} %pos_hbm.5, f32[64,512]{1,0:T(8,128)} %get-tuple-element.20.kv_hbm, bf16[64,3072]{1,0:T(8,128)(2,1)} %get-tuple-element.21.hid_hbm, ...), custom_call_target="tpu_custom_call", output_to_operand_aliasing={{1}: (5, {}), {2}: (6, {})} | custom-call | tf_op jit(solution)/shard_map/exit/pallas_call | solution.py:595

commit v5 on v4

--- a/solution.py
+++ b/solution.py
@@ -341,16 +341,18 @@
             send(stats.at[rows], mix.at[layer, kind], mix_send.at[layer, kind], mix_recv.at[layer, kind], "sp", peer)
 
     def combine(layer, stats, q_rows, kv_rows):
+        news = []
+        for h in range(HEADS):
+            k = kv_rows[:, 2 * (h // GROUP) * HEAD:(2 * (h // GROUP) + 1) * HEAD]
+            news.append(jnp.sum(q_rows[:, h * HEAD:(h + 1) * HEAD] * k, axis=-1, keepdims=True) * (1.0 / HEAD))
         for kind in range(3):
             dst = mix.at[layer, kind]
             arrived(dst, dst, mix_send.at[layer, kind], mix_recv.at[layer, kind], "sp", partners[kind])
         shards = [stats[my_rows, :]] + [mix[layer, d] for d in range(3)]
         for h in range(HEADS):
             c = h // GROUP
-            q = q_rows[:, h * HEAD:(h + 1) * HEAD]
-            k = kv_rows[:, 2 * c * HEAD:(2 * c + 1) * HEAD]
             v = kv_rows[:, (2 * c + 1) * HEAD:(2 * c + 2) * HEAD]
-            fresh = jnp.sum(q * k, axis=-1, keepdims=True) * (1.0 / HEAD)
+            fresh = news[h]
             peaks = [x[:, QW + h:QW + h + 1] for x in shards]
             top = fresh
             for peak in peaks:

time: 98.6 us -> 97.6 us (0.990)
  Pallas kernels: 97.7 us -> 96.6 us
    pallas_call x1, Pallas kernels: 78.5 us -> 77.4 us  [device_step(): pl.pallas_call(main_kernel, out_shape=(jax.ShapeDtypeStruct((SEQS, D), BF...]
where the time goes in v5:
time: 97.6 us; the launch traced here: 97.4 us
  Pallas kernels  96.6 us (99%)
    pallas_call x1, Pallas kernels, device_step(): pl.pallas_call(main_kernel, out_shape=(jax.ShapeDtypeStruct((SEQS, D), BF...  77.4 us
    pallas_call x1, Pallas kernels, device_step(): pl.pallas_call(entry_kernel, out_shape=(cache, cache, *rows), in_specs=[h...  12.1 us
    pallas_call x1, Pallas kernels, device_step(): pl.pallas_call(exit_kernel, out_shape=(jax.ShapeDtypeStruct((SEQS, D), BF...  7.09 us

profile of v5, /device:TPU:1, one launch (start us, length us, event | category | flops | bytes accessed | tf_op | source)
XLA Modules:
  0.0 97.4 jit_solution(12525006552778338235)
XLA Ops:
  0.6 12.1 %entry.1 = (bf16[2,64,256,128]{3,2,1,0:T(8,128)(2,1)}, bf16[2,64,256,128]{3,2,1,0:T(8,128)(2,1)}, f32[64,768]{1,0:T(8,128)}, f32[64,512]{1,0:T(8,128)}, f32[64,8...) custom-call(s32[64]{0:T(128)} %pos_hbm.5, bf16[64,3072]{1,0:T(8,128)(2,1)} %hidden_hbm.3, ...), custom_call_target="tpu_custom_call" | custom-call | tf_op jit(solution)/shard_map/entry/pallas_call | solution.py:548
  12.7 77.4 %main.1 = (bf16[64,3072]{1,0:T(8,128)(2,1)}, f32[64,512]{1,0:T(8,128)}) custom-call(s32[64]{0:T(128)} %pos_hbm.5, f32[64,768]{1,0:T(8,128)} %get-tuple-element.15.q0_hbm, f32[64,512]{1,0:T(8,128)} %get-tuple-element.16.kv0_hbm, f32[64,896]{1,0:T(8,128)} %get-tuple-element.17.stats0_hbm, f32[64,128]{1,0:T(8,128)} %get-tuple-element.18.cos_hbm, ...), custom_call_target="tpu_custom_call" | custom-call | tf_op jit(solution)/shard_map/main/pallas_call | solution.py:561
  90.1 7.1 %exit.1 = (bf16[64,3072]{1,0:T(8,128)(2,1)}, bf16[2,64,256,128]{3,2,1,0:T(8,128)(2,1)}, bf16[2,64,256,128]{3,2,1,0:T(8,128)(2,1)}) custom-call(s32[64]{0:T(128)} %pos_hbm.5, f32[64,512]{1,0:T(8,128)} %get-tuple-element.20.kv_hbm, bf16[64,3072]{1,0:T(8,128)(2,1)} %get-tuple-element.21.hid_hbm, ...), custom_call_target="tpu_custom_call", output_to_operand_aliasing={{1}: (5, {}), {2}: (6, {})} | custom-call | tf_op jit(solution)/shard_map/exit/pallas_call | solution.py:597
